TPU v7x, 512 devices: a whole 4x8x8 slice. The times are simulated.
512 devices in a mesh: gx: 8 (over z), gy: 4 (over x_lo, core), gz: 16 (over y, x_hi).
Axes of the slice: x: 4 (x_hi: 2, x_lo: 2; x = x_hi * 2 + x_lo), y: 8, z: 8, core: 2. Of those that a mesh axis runs over, the one named last changes fastest.
Arguments:
- probe_bits: int32 [32, 128, 512], P('gx', 'gz', 'gy'), may hold values from -2147483648 to 2147483646
- disorder_levels: int32 [32, 128, 512], P('gx', 'gz', 'gy'), may hold values from -2147483648 to 2147483647, as said below
Outputs:
- moments: float32 [3, 8], replicated
- previous: float32 [8, 32, 512, 512], P(None, 'gx', 'gz', 'gy')
- current: float32 [8, 32, 512, 512], P(None, 'gx', 'gz', 'gy')
Inputs may be any that keep to these rules, and one draw needn't show every extreme that they name: `disorder_levels`: every byte of a word is a level 0 to 255.
All inputs are finite; a program needn't handle non-finite values.
Results may differ from a plain program's by a relative error of at most 0.00002.
Values sent between devices are 32-bit elements; how exact they have to be, the bound alone decides.
No kernel may reach another device: no remote copies, remote signals or barrier semaphores. Data moves between devices by JAX's collectives and lax.ppermute only.
A program may use at most 64 MiB of HBM per device.

v0:
```python
import functools

import jax
import jax.numpy as jnp
from jax import lax
from jax.sharding import Mesh
from jax.sharding import PartitionSpec as P

PROBES = 8
LEVELS = 256
GX_GY_GZ = ("gx", "gy_0", "gy_1", "gz_0", "gz_1")
GY = ("gy_0", "gy_1")
GZ = ("gz_0", "gz_1")


disorder_width = 4.0
spectral_scale = 8.4


def with_halo(cells, sides, width):
    for axis, dim in sides:
        count = lax.axis_size(axis)
        head = lax.slice_in_dim(cells, 0, width, axis=dim)
        tail = lax.slice_in_dim(cells, cells.shape[dim] - width, cells.shape[dim], axis=dim)
        cells = jnp.concatenate(
            [
                lax.ppermute(tail, axis, [(i, (i + 1) % count) for i in range(count)]),
                cells,
                lax.ppermute(head, axis, [((i + 1) % count, i) for i in range(count)]),
            ],
            axis=dim,
        )
    return cells


def by_axis(array, axes):
    return functools.reduce(lax.psum, axes, array)


def unpack_signs(packed):
    shifts = (
        4 * jnp.arange(PROBES, dtype=jnp.int32)[:, None] + jnp.arange(4, dtype=jnp.int32)[None, :]
    )
    bit_values = jnp.right_shift(packed[None, :, :, None, :], shifts[:, None, None, :, None]) & 1
    layout = bit_values.shape
    flat = bit_values.reshape(layout[0], layout[1], layout[2] * layout[3], layout[4])
    return 2.0 * flat.astype(jnp.float32) - 1.0


def unpack_energy(packed):
    shifts = 8 * jnp.arange(4, dtype=jnp.int32)
    levels = jnp.right_shift(packed[:, :, None, :], shifts[None, None, :, None]) & 255
    layout = levels.shape
    flat = levels.reshape(layout[0], layout[1] * layout[2], layout[3])
    return disorder_width * ((flat.astype(jnp.float32) + 0.5) / LEVELS - 0.5)


def crop_sites(block, margin):
    return block[..., margin:-margin, margin:-margin, margin:-margin]


def crop_depth(block, margin):
    return block[..., margin:-margin, :]


def valid_ham(padded, energy):
    center = padded[:, 1:-1, 1:-1, 1:-1]
    beside = padded[:, 2:, 1:-1, 1:-1] + padded[:, :-2, 1:-1, 1:-1]
    beside = beside + padded[:, 1:-1, 1:-1, 2:] + padded[:, 1:-1, 1:-1, :-2]
    beside = beside + padded[:, 1:-1, 2:, 1:-1] + padded[:, 1:-1, :-2, 1:-1]
    return (energy[None] * center - beside) / spectral_scale


def per_device(probe_bits, disorder_levels):
    stacked = jnp.stack([probe_bits, disorder_levels], 0)
    extended = with_halo(stacked, (("gx", 1), (GY, 3), (GZ, 2)), 3)
    signs_wide = crop_depth(unpack_signs(extended[0]), 9)
    energy_wide = crop_depth(unpack_energy(extended[1]), 9)
    first_wide = valid_ham(signs_wide, crop_sites(energy_wide, 1))
    second_wide = 2.0 * valid_ham(first_wide, crop_sites(energy_wide, 2)) - crop_sites(
        signs_wide, 2
    )
    third = 2.0 * valid_ham(second_wide, crop_sites(energy_wide, 3)) - crop_sites(first_wide, 2)
    signs = crop_sites(signs_wide, 3)
    first = crop_sites(first_wide, 2)
    second = crop_sites(second_wide, 1)
    partial_sums = [jnp.sum(signs * vec, axis=(1, 2, 3)) for vec in (first, second, third)]
    total_sites = (
        third.shape[1]
        * third.shape[2]
        * third.shape[3]
        * lax.axis_size("gx")
        * lax.axis_size(GY)
        * lax.axis_size(GZ)
    )
    summed = [by_axis(part_sum, GX_GY_GZ) for part_sum in partial_sums]
    moments = jnp.stack(summed) / total_sites
    return (moments, second, third)


def solution(mesh):
    torus = Mesh(
        mesh.devices.reshape(mesh.shape["gx"], 2, 2, 8, 2), ("gx", "gy_0", "gy_1", "gz_0", "gz_1")
    )
    return jax.shard_map(
        per_device,
        mesh=torus,
        in_specs=(P("gx", GZ, GY), P("gx", GZ, GY)),
        out_specs=(P(), P(None, "gx", GZ, GY), P(None, "gx", GZ, GY)),
        check_vma=False,
    )
```

profile of v0, /device:TPU:6, one launch (start us, length us, event | category | flops | bytes accessed | tf_op | source)
XLA Modules:
  0.0 101.9 jit_solution(648168939208347832)
XLA Ops:
  0.6 0.8 fusion.7
  1.4 4.3 %collective-permute-start = (s32[2,3,8,128]{3,2,1,0:T(8,128)S(1)}, s32[2,3,8,128]{3,2,1,0:T(8,128)S(1)}, u32[]{:S(2)}, u32[]{:S(2)}) collective-permute-start(s32[2,3,8,128]{3,2,1,0:T(8,128)S(1)} %get-tuple-element.29), channel_id=1, source_target_pairs={{0,64},{64,128},{128,192},{192,256},{256,320},{320,384},{384,448},... | collective-permute-start | bytes 73736 | tf_op jit(solution)/shard_map/ppermute | solution.py:27
  5.7 8.6 %collective-permute-start.1 = (s32[2,3,8,128]{3,2,1,0:T(8,128)S(1)}, s32[2,3,8,128]{3,2,1,0:T(8,128)S(1)}, u32[]{:S(2)}, u32[]{:S(2)}) collective-permute-start(s32[2,3,8,128]{3,2,1,0:T(8,128)S(1)} %get-tuple-element.30), channel_id=1, source_target_pairs={{64,0},{128,64},{192,128},{256,192},{320,256},{384,320},{448,384},... | collective-permute-start | bytes 73736 | tf_op jit(solution)/shard_map/ppermute | solution.py:29
  14.3 1.5 %collective-permute-done.1 = s32[2,3,8,128]{3,2,1,0:T(8,128)S(1)} collective-permute-done((s32[2,3,8,128]{3,2,1,0:T(8,128)S(1)}, s32[2,3,8,128]{3,2,1,0:T(8,128)S(1)}, u32[]{:S(2)}, u32[]{:S(2)}) %collective-permute-start.1) | collective-permute-done | bytes 24608 | tf_op jit(solution)/shard_map/ppermute | solution.py:29
  15.8 0.7 pad_add_fusion.2
  16.6 1.9 %collective-permute-start.2 = (s32[2,10,8,3]{3,2,1,0:T(8,128)S(1)}, s32[2,10,8,3]{3,2,1,0:T(8,128)S(1)}, u32[]{:S(2)}, u32[]{:S(2)}) collective-permute-start(s32[2,10,8,3]{3,2,1,0:T(8,128)S(1)} %get-tuple-element.27), channel_id=1, source_target_pairs={{0,16},{16,32},{32,48},{48,0},{1,17},{17,33},{33,49},{49,1},{2,18}... | collective-permute-start | bytes 5768 | tf_op jit(solution)/shard_map/ppermute | solution.py:27
  18.5 3.6 %collective-permute-start.3 = (s32[2,10,8,3]{3,2,1,0:T(8,128)S(1)}, s32[2,10,8,3]{3,2,1,0:T(8,128)S(1)}, u32[]{:S(2)}, u32[]{:S(2)}) collective-permute-start(s32[2,10,8,3]{3,2,1,0:T(8,128)S(1)} %get-tuple-element.28), channel_id=1, source_target_pairs={{16,0},{32,16},{48,32},{0,48},{17,1},{33,17},{49,33},{1,49},{18,2}... | collective-permute-start | bytes 5768 | tf_op jit(solution)/shard_map/ppermute | solution.py:29
  22.4 1.9 %collective-permute-done.3 = s32[2,10,8,3]{3,2,1,0:T(8,128)S(1)} collective-permute-done((s32[2,10,8,3]{3,2,1,0:T(8,128)S(1)}, s32[2,10,8,3]{3,2,1,0:T(8,128)S(1)}, u32[]{:S(2)}, u32[]{:S(2)}) %collective-permute-start.3) | collective-permute-done | bytes 1952 | tf_op jit(solution)/shard_map/ppermute | solution.py:29
  24.2 0.9 pad_add_fusion.1
  25.1 4.3 %collective-permute-start.4 = (s32[2,10,3,134]{3,2,1,0:T(4,128)S(1)}, s32[2,10,3,134]{3,2,1,0:T(4,128)S(1)}, u32[]{:S(2)}, u32[]{:S(2)}) collective-permute-start(s32[2,10,3,134]{3,2,1,0:T(4,128)S(1)} %get-tuple-element.25), channel_id=1, source_target_pairs={{0,1},{1,2},{2,3},{3,4},{4,5},{5,6},{6,7},{7,8},{8,9},{9,10},{10,1... | collective-permute-start | bytes 96488 | tf_op jit(solution)/shard_map/ppermute | solution.py:27
  29.5 3.0 %collective-permute-start.5 = (s32[2,10,3,134]{3,2,1,0:T(4,128)S(1)}, s32[2,10,3,134]{3,2,1,0:T(4,128)S(1)}, u32[]{:S(2)}, u32[]{:S(2)}) collective-permute-start(s32[2,10,3,134]{3,2,1,0:T(4,128)S(1)} %get-tuple-element.26), channel_id=1, source_target_pairs={{1,0},{2,1},{3,2},{4,3},{5,4},{6,5},{7,6},{8,7},{9,8},{10,9},{11,1... | collective-permute-start | bytes 96488 | tf_op jit(solution)/shard_map/ppermute | solution.py:29
  32.7 1.1 %collective-permute-done.4 = s32[2,10,3,134]{3,2,1,0:T(4,128)S(1)} collective-permute-done((s32[2,10,3,134]{3,2,1,0:T(4,128)S(1)}, s32[2,10,3,134]{3,2,1,0:T(4,128)S(1)}, u32[]{:S(2)}, u32[]{:S(2)}) %collective-permute-start.4) | collective-permute-done | bytes 32192 | tf_op jit(solution)/shard_map/ppermute | solution.py:27
  33.8 4.7 %collective-permute-done.5 = s32[2,10,3,134]{3,2,1,0:T(4,128)S(1)} collective-permute-done((s32[2,10,3,134]{3,2,1,0:T(4,128)S(1)}, s32[2,10,3,134]{3,2,1,0:T(4,128)S(1)}, u32[]{:S(2)}, u32[]{:S(2)}) %collective-permute-start.5) | collective-permute-done | bytes 32192 | tf_op jit(solution)/shard_map/ppermute | solution.py:29
  38.6 0.9 pad_add_fusion
  40.7 0.8 multiply_add_fusion
  41.5 4.5 %fusion.1 = f32[8,8,36,132]{3,2,1,0:T(8,128)S(1)} fusion(f32[8,10,56,134]{3,2,1,0:T(8,128)S(1)} %multiply_add_fusion, f32[8,36,132]{2,1,0:T(8,128)S(1)} %slice.165), kind=kLoop, calls=%fused_computation.3 | loop fusion | flops 2433024 | bytes 9884160 | tf_op jit(solution)/shard_map/div | solution.py:71
  46.1 3.6 %slice_subtract_fusion = f32[8,6,34,130]{3,2,1,0:T(8,128)S(1)} fusion(f32[8,10,56,134]{3,2,1,0:T(8,128)S(1)} %multiply_add_fusion, f32[8,8,36,132]{3,2,1,0:T(8,128)S(1)} %fusion.1, f32[6,34,130]{2,1,0:T(8,128)S(1)} %slice.174), kind=kLoop, calls=%fused_computation.9 | loop fusion | flops 1909440 | bytes 7743840 | tf_op jit(solution)/shard_map/sub | solution.py:80
  49.7 2.1 %multiply_reduce_fusion.2 = (f32[8]{0:T(128)S(1)}, f32[8]{0:T(128)S(1)}, f32[8]{0:T(128)S(1)}, f32[8,4,32,128]{3,2,1,0:T(8,128)}, f32[8,4,32,128]{3,2,1,0:T(8,128)}) fusion(f32[8,8,36,132]{3,2,1,0:T(8,128)S(1)} %fusion.1, f32[8,10,56,134]{3,2,1,0:T(8,128)S(1)} %multiply_add_fusion, f32[8,6,34,130]{3,2,1,0:T(8,128)S(1)} %slice_subtract_fusion, ...), kind=kLoop, calls=%fused_computation.29 | loop fusion | flops 1966056 | bytes 5832800 | tf_op jit(solution)/shard_map/reduce_sum | solution.py:87
  51.9 17.6 %all-reduce.1 = (f32[8]{0:T(128)S(1)}, f32[8]{0:T(128)S(1)}, f32[8]{0:T(128)S(1)}) all-reduce(f32[8]{0:T(128)S(1)} %get-tuple-element.5, f32[8]{0:T(128)S(1)} %get-tuple-element.4, f32[8]{0:T(128)S(1)} %get-tuple-element.3), channel_id=1, replica_groups=mesh['gx'=8,'gy_0'=2,'gy_1'=2,'gz_0'=8,'gz_1'=2] {'gx'}, use_global_device_ids=true, to_apply=%region_13.0 | all-reduce | flops 24 | bytes 192 | tf_op jit(solution)/shard_map/psum | solution.py:37
  69.5 4.9 %all-reduce.4 = (f32[8]{0:T(128)S(1)}, f32[8]{0:T(128)S(1)}, f32[8]{0:T(128)S(1)}) all-reduce(f32[8]{0:T(128)S(1)} %get-tuple-element.9, f32[8]{0:T(128)S(1)} %get-tuple-element.10, f32[8]{0:T(128)S(1)} %get-tuple-element.11), channel_id=1, replica_groups=mesh['gx'=8,'gy_0'=2,'gy_1'=2,'gz_0'=8,'gz_1'=2] {'gy_0'}, use_global_device_ids=true, to_apply=%region_14.0 | all-reduce | flops 24 | bytes 192 | tf_op jit(solution)/shard_map/psum | solution.py:37
  74.4 2.4 %all-reduce.3 = (f32[8]{0:T(128)S(1)}, f32[8]{0:T(128)S(1)}, f32[8]{0:T(128)S(1)}) all-reduce(f32[8]{0:T(128)S(1)} %get-tuple-element.18, f32[8]{0:T(128)S(1)} %get-tuple-element.19, f32[8]{0:T(128)S(1)} %get-tuple-element.20), channel_id=1, replica_groups=mesh['gx'=8,'gy_0'=2,'gy_1'=2,'gz_0'=8,'gz_1'=2] {'gy_1'}, use_global_device_ids=true, to_apply=%region_15.0 | all-reduce | flops 24 | bytes 192 | tf_op jit(solution)/shard_map/psum | solution.py:37
  76.9 18.0 %all-reduce = (f32[8]{0:T(128)S(1)}, f32[8]{0:T(128)S(1)}, f32[8]{0:T(128)S(1)}) all-reduce(f32[8]{0:T(128)S(1)} %get-tuple-element.15, f32[8]{0:T(128)S(1)} %get-tuple-element.16, f32[8]{0:T(128)S(1)} %get-tuple-element.17), channel_id=1, replica_groups=mesh['gx'=8,'gy_0'=2,'gy_1'=2,'gz_0'=8,'gz_1'=2] {'gz_0'}, use_global_device_ids=true, to_apply=%region_16.0 | all-reduce | flops 24 | bytes 192 | tf_op jit(solution)/shard_map/psum | solution.py:37
  94.9 6.4 %all-reduce.2 = (f32[1,8]{1,0:T(1,128)S(1)}, f32[1,8]{1,0:T(1,128)S(1)}, f32[1,8]{1,0:T(1,128)S(1)}) all-reduce(f32[1,8]{1,0:T(1,128)S(1)} %bitcast.19, f32[1,8]{1,0:T(1,128)S(1)} %bitcast.20, f32[1,8]{1,0:T(1,128)S(1)} %bitcast.21), channel_id=1, replica_groups=mesh['gx'=8,'gy_0'=2,'gy_1'=2,'gz_0'=8,'gz_1'=2] {'gz_1'}, use_global_device_ids=true, to_apply=%region_17.0 | all-reduce | flops 24 | bytes 192 | tf_op jit(solution)/shard_map/psum | solution.py:37
  101.4 0.6 maximum_multiply_fusion
  (20 shorter events, 1.6 us)
Async XLA Ops:
  1.4 12.9 %collective-permute-start = (s32[2,3,8,128]{3,2,1,0:T(8,128)S(1)}, s32[2,3,8,128]{3,2,1,0:T(8,128)S(1)}, u32[]{:S(2)}, u32[]{:S(2)}) collective-permute-start(s32[2,3,8,128]{3,2,1,0:T(8,128)S(1)} %get-tuple-element.29), channel_id=1, source_target_pairs={{0,64},{64,128},{128,192},{192,256},{256,320},{320,384},{384,448},... | collective-permute-start | bytes 73736 | tf_op jit(solution)/shard_map/ppermute | solution.py:27
  5.7 10.1 %collective-permute-start.1 = (s32[2,3,8,128]{3,2,1,0:T(8,128)S(1)}, s32[2,3,8,128]{3,2,1,0:T(8,128)S(1)}, u32[]{:S(2)}, u32[]{:S(2)}) collective-permute-start(s32[2,3,8,128]{3,2,1,0:T(8,128)S(1)} %get-tuple-element.30), channel_id=1, source_target_pairs={{64,0},{128,64},{192,128},{256,192},{320,256},{384,320},{448,384},... | collective-permute-start | bytes 73736 | tf_op jit(solution)/shard_map/ppermute | solution.py:29
  16.6 5.8 %collective-permute-start.2 = (s32[2,10,8,3]{3,2,1,0:T(8,128)S(1)}, s32[2,10,8,3]{3,2,1,0:T(8,128)S(1)}, u32[]{:S(2)}, u32[]{:S(2)}) collective-permute-start(s32[2,10,8,3]{3,2,1,0:T(8,128)S(1)} %get-tuple-element.27), channel_id=1, source_target_pairs={{0,16},{16,32},{32,48},{48,0},{1,17},{17,33},{33,49},{49,1},{2,18}... | collective-permute-start | bytes 5768 | tf_op jit(solution)/shard_map/ppermute | solution.py:27
  18.5 5.7 %collective-permute-start.3 = (s32[2,10,8,3]{3,2,1,0:T(8,128)S(1)}, s32[2,10,8,3]{3,2,1,0:T(8,128)S(1)}, u32[]{:S(2)}, u32[]{:S(2)}) collective-permute-start(s32[2,10,8,3]{3,2,1,0:T(8,128)S(1)} %get-tuple-element.28), channel_id=1, source_target_pairs={{16,0},{32,16},{48,32},{0,48},{17,1},{33,17},{49,33},{1,49},{18,2}... | collective-permute-start | bytes 5768 | tf_op jit(solution)/shard_map/ppermute | solution.py:29
  25.1 8.7 %collective-permute-start.4 = (s32[2,10,3,134]{3,2,1,0:T(4,128)S(1)}, s32[2,10,3,134]{3,2,1,0:T(4,128)S(1)}, u32[]{:S(2)}, u32[]{:S(2)}) collective-permute-start(s32[2,10,3,134]{3,2,1,0:T(4,128)S(1)} %get-tuple-element.25), channel_id=1, source_target_pairs={{0,1},{1,2},{2,3},{3,4},{4,5},{5,6},{6,7},{7,8},{8,9},{9,10},{10,1... | collective-permute-start | bytes 96488 | tf_op jit(solution)/shard_map/ppermute | solution.py:27
  29.5 9.1 %collective-permute-start.5 = (s32[2,10,3,134]{3,2,1,0:T(4,128)S(1)}, s32[2,10,3,134]{3,2,1,0:T(4,128)S(1)}, u32[]{:S(2)}, u32[]{:S(2)}) collective-permute-start(s32[2,10,3,134]{3,2,1,0:T(4,128)S(1)} %get-tuple-element.26), channel_id=1, source_target_pairs={{1,0},{2,1},{3,2},{4,3},{5,4},{6,5},{7,6},{8,7},{9,8},{10,9},{11,1... | collective-permute-start | bytes 96488 | tf_op jit(solution)/shard_map/ppermute | solution.py:29
where the time goes:
time: 103 us; the launch traced here: 102 us
  blocking collectives  49.5 us (48%)
  starting transfers between devices  25.8 us (25%)
  other arithmetic  15.2 us (15%)
  waiting for transfers between devices  9.37 us (9%)
  local copies, waits for them, and re-layouts  1.25 us (1%)
    psum x5, blocking collectives, by_axis(): return functools.reduce(lax.psum, axes, array)  49.5 us
    ppermute x3, starting transfers between devices, with_halo(): lax.ppermute(head, axis, [((i + 1) % count, i) for i in range(count)])  15.2 us
    ppermute x3, starting transfers between devices, with_halo(): lax.ppermute(tail, axis, [(i, (i + 1) % count) for i in range(count)])  10.5 us
    ppermute x3, waiting for transfers between devices, with_halo(): lax.ppermute(head, axis, [((i + 1) % count, i) for i in range(count)])  8.07 us
    div x1, other arithmetic, valid_ham(): return (energy[None] * center - beside) / spectral_scale  4.54 us
    sub x1, other arithmetic, per_device(): 2.0 * valid_ham(first_wide, crop_sites(energy_wide, 2))  3.64 us
    concatenate x3, other arithmetic, with_halo(): jnp.concatenate([lax.ppermute(tail, axis, [(i, (i + 1) % count) for i in...  2.53 us
    reduce_sum x1, other arithmetic, per_device(): jnp.sum(signs * vec, axis=(1, 2, 3))  2.12 us
  transfers between devices with their start and end apart: 6, of which 5 were waited for; matrix products, arithmetic and copies ran while one was open for 0% of the time, Pallas kernels for 0%

commit v1 on v0

v1 whole, which is shorter than its diff:
```python
import functools

import jax
import jax.numpy as jnp
from jax import lax
from jax.experimental import pallas as pl
from jax.experimental.pallas import tpu as pltpu
from jax.sharding import Mesh
from jax.sharding import PartitionSpec as P

PROBES = 8
LEVELS = 256
NX, NW, NY = 4, 8, 128
NZ = 4 * NW
GY = ("ya", "yb")
GZ = ("za", "zb")
NEAR = ("gx", "ya", "yb", "zb")
FAR = "za"

disorder_width = 4.0
spectral_scale = 8.4
INV = 1.0 / spectral_scale
TWO = 2.0 / spectral_scale
E_MUL = TWO * disorder_width / LEVELS
E_ADD = TWO * disorder_width * (0.5 / LEVELS - 0.5)

PLANES = 18
ROWS = 24


def vmem(n):
    return [pl.BlockSpec(memory_space=pltpu.VMEM)] * n


def lanes(shape):
    return lax.broadcasted_iota(jnp.int32, shape, len(shape) - 1)


def edge_kernel(bits, levels, out):
    lane = lanes((NW, NY))
    word = lax.broadcasted_iota(jnp.int32, (NW, NY), 0)
    mask = (lane // 16 == word) & (lane % 16 < 6)
    for a, src in enumerate((bits, levels)):
        for x in range(NX):
            rolled = pltpu.roll(src[x], 3, 1, stride=16, stride_axis=0)
            out[a * NX + x : a * NX + x + 1] = jnp.sum(
                jnp.where(mask, rolled, 0), axis=0, keepdims=True
            )


def face_kernel(where, bits, levels, left, right, edges, low, high):
    del where
    lane = lanes((NW, NY))
    both = jnp.where(lane % 16 < 3, left[...], right[...])
    edges[...] = both
    for out, first in ((low, 0), (high, 1)):
        for i in range(3):
            out[8 * i : 8 * i + 8] = bits[first + i]
        for i in range(2):
            out[24 + 8 * i : 32 + 8 * i] = levels[2 * first + i]
        out[40:48] = both


def plane_list(bits, levels, edges, below, above):
    found = []
    for x in range(-3, 7):
        if x < 0:
            found.append((below, 8 * (x + 3), below, 40 + x + 4))
        elif x < NX:
            found.append((bits, x, edges, x))
        else:
            found.append((above, 8 * (x - 4), above, 40 + x - 4))
    for x in range(-2, 6):
        if x < 0:
            found.append((below, 24 + 8 * (x + 2), below, 44 + x + 4))
        elif x < NX:
            found.append((levels, x, edges, 4 + x))
        else:
            found.append((above, 24 + 8 * (x - 4), above, 44 + x - 4))
    return found


def word_row(plane, w):
    ref, at = plane[:2]
    if len(ref.shape) == 3:
        return ref[at, w : w + 1, :]
    return ref[at + w : at + w + 1, :]


def shift_edges(rows, w):
    return pltpu.roll(rows, (-(16 * w + 3)) % NY, 1)


def level_kernel(bits, levels, edges, below, above, low, high, strip):
    planes = plane_list(bits, levels, edges, below, above)
    strip[PLANES - PLANES % 8 :] = jnp.zeros((8, NY), jnp.int32)
    for k, plane in enumerate(planes):
        strip[k : k + 1] = plane[2][plane[3] : plane[3] + 1, :]
    for out, w in ((low, 0), (high, NW - 1)):
        out[16:24] = jnp.zeros((8, NY), jnp.int32)
        for k, plane in enumerate(planes):
            out[k : k + 1] = word_row(plane, w)
        out[ROWS:] = shift_edges(strip[...], w)


def field_kernel(
    bits, levels, edges, below, above, under, over,
    previous, current, message,
    strip, borders, v0, energy, v1, v2,
):
    planes = plane_list(bits, levels, edges, below, above)
    strip[16:24] = jnp.zeros((8, NY), jnp.int32)
    for k, plane in enumerate(planes):
        strip[k : k + 1] = plane[2][plane[3] : plane[3] + 1, :]
    for w in range(NW):
        borders[w] = shift_edges(strip[...], w)

    tile = (PROBES, NY)
    probe = lax.broadcasted_iota(jnp.int32, tile, 0)
    lane = lanes(tile)
    bit_of = [jnp.left_shift(1, 4 * probe + j) for j in range(4)]
    first_lane, last_lane = lane == 0, lane == NY - 1

    def rows_of(k, w):
        if w < 0:
            pair = under[k : k + 1, :], under[ROWS + k : ROWS + k + 1, :]
        elif w >= NW:
            pair = over[k : k + 1, :], over[ROWS + k : ROWS + k + 1, :]
        else:
            pair = word_row(planes[k], w), borders[w, k : k + 1, :]
        return [jnp.broadcast_to(row, tile) for row in pair]

    for k in range(10):
        for w in range(-1, NW + 1):
            for half, row in enumerate(rows_of(k, w)):
                for j in range(4):
                    z = 4 * w + j
                    if -3 <= z < NZ + 3:
                        v0[k, z + 3, :, NY * half : NY * (half + 1)] = jnp.where(
                            (row & bit_of[j]) != 0, 1.0, -1.0
                        )
    for k in range(8):
        for w in range(-1, NW + 1):
            for half, row in enumerate(rows_of(10 + k, w)):
                for j in range(4):
                    z = 4 * w + j
                    if -2 <= z < NZ + 2:
                        level = jnp.right_shift(row, 8 * j) & 255
                        energy[k, z + 2, :, NY * half : NY * (half + 1)] = (
                            level.astype(jnp.float32) * E_MUL + E_ADD
                        )

    def get(ref, x, z):
        return ref[x, z, :, :NY], ref[x, z, :, NY:]

    def step(ref, x, z, ex, ez, main_only=False):
        m, e = get(ref, x, z)
        up_m, up_e = pltpu.roll(m, NY - 1, 1), pltpu.roll(e, NY - 1, 1)
        dn_m, dn_e = pltpu.roll(m, 1, 1), pltpu.roll(e, 1, 1)
        beside = [jnp.where(last_lane, up_e, up_m) + jnp.where(first_lane, dn_e, dn_m)]
        if not main_only:
            beside.append(jnp.where(last_lane, up_m, up_e) + jnp.where(first_lane, dn_m, dn_e))
        result = []
        for half, s in enumerate(beside):
            at = slice(NY * half, NY * (half + 1))
            s = s + (ref[x + 1, z, :, at] + ref[x - 1, z, :, at])
            s = s + (ref[x, z + 1, :, at] + ref[x, z - 1, :, at])
            result.append(energy[ex, ez, :, at] * (m, e)[half] - TWO * s)
        return result

    UNROLL = 4
    for x in range(8):

        def first(i, carry, x=x):
            for u in range(UNROLL):
                z = i * UNROLL + u
                for half, t in enumerate(step(v0, x + 1, z + 1, x, z)):
                    v1[x, z, :, NY * half : NY * (half + 1)] = 0.5 * t
            return carry

        lax.fori_loop(0, (NZ + 4) // UNROLL, first, 0)

    for x in range(6):

        def second(i, carry, x=x):
            for u in range(2):
                z = i * 2 + u
                for half, t in enumerate(step(v1, x + 1, z + 1, x + 1, z + 1)):
                    at = slice(NY * half, NY * (half + 1))
                    v2[x, z, :, at] = t - v0[x + 2, z + 2, :, at]
            return carry

        lax.fori_loop(0, (NZ + 2) // 2, second, 0)

    sums = [jnp.zeros(tile, jnp.float32)] * 3
    for x in range(NX):

        def third(i, sums, x=x):
            sums = list(sums)
            for u in range(UNROLL):
                z = i * UNROLL + u
                t = step(v2, x + 1, z + 1, x + 2, z + 2, main_only=True)[0]
                one = v1[x + 2, z + 2, :, :NY]
                two = v2[x + 1, z + 1, :, :NY]
                three = t - one
                previous[pl.ds(x * NZ + z, PROBES, stride=NX * NZ), :] = two
                current[pl.ds(x * NZ + z, PROBES, stride=NX * NZ), :] = three
                sign = v0[x + 3, z + 3, :, :NY]
                sums = [acc + sign * v for acc, v in zip(sums, (one, two, three))]
            return tuple(sums)

        sums = lax.fori_loop(0, NZ // UNROLL, third, tuple(sums))

    row = jnp.zeros(tile, jnp.float32)
    for n, acc in enumerate(sums):
        total = jnp.sum(acc, axis=1, keepdims=True)
        row = jnp.where(lane == 8 * n + probe, total, row)
    row = jnp.sum(row, axis=0, keepdims=True)
    message[...] = jnp.broadcast_to(row, message.shape)


def shape(rows, dtype=jnp.int32):
    return jax.ShapeDtypeStruct(rows, dtype)


def shift(array, axis, by):
    count = lax.axis_size(axis)
    return lax.ppermute(array, axis, [(i, (i + by) % count) for i in range(count)])


def per_device(bits, levels):
    tile = (NW, NY)
    edge = pl.pallas_call(
        edge_kernel, out_shape=shape(tile), in_specs=vmem(2), out_specs=vmem(1)[0], name="edge"
    )(bits, levels)
    gathered = lax.all_gather(edge, GY)
    count = lax.axis_size(GY)
    here = lax.axis_index(GY)
    where = jnp.stack([(here + count - 1) % count, (here + 1) % count]).astype(jnp.int32)
    whole = pl.BlockSpec((NX, NW, NY), lambda i, w: (0, 0, 0))
    flat = lambda rows: pl.BlockSpec((rows, NY), lambda i, w: (0, 0))
    edges, low, high = pl.pallas_call(
        face_kernel,
        out_shape=(shape(tile), shape((48, NY)), shape((48, NY))),
        grid_spec=pltpu.PrefetchScalarGridSpec(
            num_scalar_prefetch=1,
            grid=(1,),
            in_specs=[
                whole,
                whole,
                pl.BlockSpec((None, NW, NY), lambda i, w: (w[0], 0, 0)),
                pl.BlockSpec((None, NW, NY), lambda i, w: (w[1], 0, 0)),
            ],
            out_specs=[flat(NW), flat(48), flat(48)],
        ),
        name="face",
    )(where, bits, levels, gathered, gathered)
    below = shift(high, "gx", 1)
    above = shift(low, "gx", -1)
    z_low, z_high = pl.pallas_call(
        level_kernel,
        out_shape=(shape((2 * ROWS, NY)),) * 2,
        in_specs=vmem(5),
        out_specs=tuple(vmem(2)),
        scratch_shapes=[pltpu.VMEM((ROWS, NY), jnp.int32)],
        name="level",
    )(bits, levels, edges, below, above)
    under = shift(z_high, GZ, 1)
    over = shift(z_low, GZ, -1)
    near = 1
    for axis in NEAR:
        near *= lax.axis_size(axis)
    far = lax.axis_size(FAR)
    total = near * far * NX * NZ * NY
    f32 = jnp.float32
    previous, current, message = pl.pallas_call(
        field_kernel,
        out_shape=(
            shape((PROBES * NX * NZ, NY), f32),
            shape((PROBES * NX * NZ, NY), f32),
            shape((near, NY), f32),
        ),
        in_specs=vmem(7),
        out_specs=tuple(vmem(3)),
        scratch_shapes=[
            pltpu.VMEM((ROWS, NY), jnp.int32),
            pltpu.VMEM((NW, ROWS, NY), jnp.int32),
            pltpu.VMEM((NX + 6, NZ + 6, PROBES, 2 * NY), f32),
            pltpu.VMEM((NX + 4, NZ + 4, PROBES, 2 * NY), f32),
            pltpu.VMEM((NX + 4, NZ + 4, PROBES, 2 * NY), f32),
            pltpu.VMEM((NX + 2, NZ + 2, PROBES, 2 * NY), f32),
        ],
        name="field",
    )(bits, levels, edges, below, above, under, over)
    part = jnp.sum(lax.all_to_all(message, NEAR, 0, 0, tiled=True), axis=0, keepdims=True)
    spread = jnp.broadcast_to(part, (far, NY))
    summed = jnp.sum(lax.all_to_all(spread, FAR, 0, 0, tiled=True), axis=0)
    moments = summed[: 3 * PROBES].reshape(3, PROBES) / total
    block = (PROBES, NX, NZ, NY)
    return moments, previous.reshape(block), current.reshape(block)


def solution(mesh):
    sizes = mesh.shape["gx"], mesh.shape["gy"], mesh.shape["gz"]
    torus = Mesh(
        mesh.devices.reshape(sizes[0], sizes[1] // 2, 2, sizes[2] // 2, 2),
        ("gx",) + GY + GZ,
    )
    return jax.shard_map(
        per_device,
        mesh=torus,
        in_specs=(P("gx", GZ, GY), P("gx", GZ, GY)),
        out_specs=(P(), P(None, "gx", GZ, GY), P(None, "gx", GZ, GY)),
        check_vma=False,
    )
```

time: 103 us -> 94.5 us (0.917)
  the two profiles are of different devices: /device:TPU:6 before, /device:TPU:1 now
where the time goes in v1:
time: 94.5 us; the launch traced here: 93.8 us
  blocking collectives  45.5 us (48%)
  Pallas kernels  25.3 us (27%)
  starting transfers between devices  17.1 us (18%)
  waiting for transfers between devices  2.55 us (3%)
  local copies, waits for them, and re-layouts  1.88 us (2%)
    pallas_call x1, Pallas kernels, per_device(): pl.pallas_call(field_kernel, out_shape=(shape((PROBES * NX * NZ, NY), f32...  20.3 us
    all_to_all x1, blocking collectives, per_device(): lax.all_to_all(message, NEAR, 0, 0, tiled=True)  19.6 us
    ppermute x4, starting transfers between devices, shift(): lax.ppermute(array, axis, [(i, (i + by) % count) for i in range(count)])  17.1 us
    all_to_all x1, blocking collectives, per_device(): summed = jnp.sum(lax.all_to_all(spread, FAR, 0, 0, tiled=True), axis=0)  13.4 us
    all_gather x1, blocking collectives, per_device(): gathered = lax.all_gather(edge, GY)  12.5 us
    ppermute x4, waiting for transfers between devices, shift(): lax.ppermute(array, axis, [(i, (i + by) % count) for i in range(count)])  2.55 us
    pallas_call x1, Pallas kernels, per_device(): pl.pallas_call(face_kernel, out_shape=(shape(tile), shape((48, NY)), shap...  2.02 us
  transfers between devices with their start and end apart: 4, of which 2 were waited for; matrix products, arithmetic and copies ran while one was open for 0% of the time, Pallas kernels for 0%

profile of v1, /device:TPU:1, one launch (start us, length us, event | category | flops | bytes accessed | tf_op | source)
XLA Modules:
  0.0 93.8 jit_solution(15411337990914269313)
XLA Ops:
  0.6 1.4 %edge.1 = s32[8,128]{1,0:T(8,128)} custom-call(s32[4,8,128]{2,1,0:T(8,128)} %bits.7, s32[4,8,128]{2,1,0:T(8,128)} %levels.7), custom_call_target="tpu_custom_call" | custom-call | tf_op jit(solution)/shard_map/edge/pallas_call | solution.py:233
  2.1 12.5 %all-gather = s32[32,128]{1,0:T(8,128)} all-gather(s32[8,128]{1,0:T(8,128)} %edge.1), channel_id=2, replica_groups=mesh['gx'=8,'ya'=2,'yb'=2,'za'=8,'zb'=2] {'ya','yb'}, dimensions={0}, use_global_device_ids=true | all-gather | bytes 20480 | tf_op jit(solution)/shard_map/all_gather | solution.py:236
  14.6 0.7 pad_add_fusion.where
  15.2 2.0 %face.1 = (s32[8,128]{1,0:T(8,128)}, s32[48,128]{1,0:T(8,128)}, s32[48,128]{1,0:T(8,128)}) custom-call(s32[2]{0:T(128)} %pad_add_fusion.where, s32[4,8,128]{2,1,0:T(8,128)} %bits.7, s32[4,8,128]{2,1,0:T(8,128)} %levels.7, s32[4,8,128]{2,1,0:T(8,128)} %bitcast.9, s32[4,8,128]{2,1,0:T(8,128)} %bitcast.10), custom_call_target="tpu_custom_call" | custom-call | tf_op jit(solution)/shard_map/face/pallas_call | solution.py:242
  17.2 1.9 %collective-permute-start = (s32[48,128]{1,0:T(8,128)}, s32[48,128]{1,0:T(8,128)S(1)}, u32[]{:S(2)}, u32[]{:S(2)}) collective-permute-start(s32[48,128]{1,0:T(8,128)} %get-tuple-element.12), channel_id=1, source_target_pairs={{0,64},{64,128},{128,192},{192,256},{256,320},{320,384},{384,448},... | collective-permute-start | bytes 73736 | tf_op jit(solution)/shard_map/ppermute | solution.py:228
  19.2 6.1 %collective-permute-start.1 = (s32[48,128]{1,0:T(8,128)}, s32[48,128]{1,0:T(8,128)S(1)}, u32[]{:S(2)}, u32[]{:S(2)}) collective-permute-start(s32[48,128]{1,0:T(8,128)} %get-tuple-element.13), channel_id=1, source_target_pairs={{0,448},{64,0},{128,64},{192,128},{256,192},{320,256},{384,320},{4... | collective-permute-start | bytes 73736 | tf_op jit(solution)/shard_map/ppermute | solution.py:228
  25.2 0.0 collective-permute-done.below
  25.2 0.0 copy-start
  25.3 1.1 %collective-permute-done.1.above = s32[48,128]{1,0:T(8,128)S(1)} collective-permute-done((s32[48,128]{1,0:T(8,128)}, s32[48,128]{1,0:T(8,128)S(1)}, u32[]{:S(2)}, u32[]{:S(2)}) %collective-permute-start.1) | collective-permute-done | bytes 24608 | tf_op jit(solution)/shard_map/ppermute | solution.py:228
  26.4 0.0 copy-done
  26.4 0.6 copy-done.1
  27.0 1.5 %level.1 = (s32[48,128]{1,0:T(8,128)}, s32[48,128]{1,0:T(8,128)}) custom-call(s32[4,8,128]{2,1,0:T(8,128)} %bits.7, s32[4,8,128]{2,1,0:T(8,128)} %levels.7, s32[8,128]{1,0:T(8,128)} %get-tuple-element.11.edges, s32[48,128]{1,0:T(8,128)} %copy-done, s32[48,128]{1,0:T(8,128)} %copy-done.1), custom_call_target="tpu_custom_call" | custom-call | tf_op jit(solution)/shard_map/level/pallas_call | solution.py:260
  28.5 4.3 %collective-permute-start.2 = (s32[48,128]{1,0:T(8,128)}, s32[48,128]{1,0:T(8,128)S(1)}, u32[]{:S(2)}, u32[]{:S(2)}) collective-permute-start(s32[48,128]{1,0:T(8,128)} %get-tuple-element.14), channel_id=1, source_target_pairs={{0,1},{1,2},{2,3},{3,4},{4,5},{5,6},{6,7},{7,8},{8,9},{9,10},{10,1... | collective-permute-start | bytes 73736 | tf_op jit(solution)/shard_map/ppermute | solution.py:228
  32.8 4.8 %collective-permute-start.3 = (s32[48,128]{1,0:T(8,128)}, s32[48,128]{1,0:T(8,128)S(1)}, u32[]{:S(2)}, u32[]{:S(2)}) collective-permute-start(s32[48,128]{1,0:T(8,128)} %get-tuple-element.15), channel_id=1, source_target_pairs={{0,15},{1,0},{2,1},{3,2},{4,3},{5,4},{6,5},{7,6},{8,7},{9,8},{10,9... | collective-permute-start | bytes 73736 | tf_op jit(solution)/shard_map/ppermute | solution.py:228
  37.6 0.0 collective-permute-done.2.under
  37.7 0.0 copy-start.2
  37.7 1.4 %collective-permute-done.3.over = s32[48,128]{1,0:T(8,128)S(1)} collective-permute-done((s32[48,128]{1,0:T(8,128)}, s32[48,128]{1,0:T(8,128)S(1)}, u32[]{:S(2)}, u32[]{:S(2)}) %collective-permute-start.3) | collective-permute-done | bytes 24608 | tf_op jit(solution)/shard_map/ppermute | solution.py:228
  39.1 0.0 copy-done.2
  39.1 0.6 copy-done.3
  39.7 20.3 %field.1 = (f32[1024,128]{1,0:T(8,128)}, f32[1024,128]{1,0:T(8,128)}, f32[64,128]{1,0:T(8,128)}) custom-call(s32[4,8,128]{2,1,0:T(8,128)} %bits.7, s32[4,8,128]{2,1,0:T(8,128)} %levels.7, s32[8,128]{1,0:T(8,128)} %get-tuple-element.11.edges, s32[48,128]{1,0:T(8,128)} %copy-done, s32[48,128]{1,0:T(8,128)} %copy-done.1, s32[48,128]{1,0:T(8,128)} %copy-done.2, ...), custom_call_target="tpu_custom_call" | custom-call | tf_op jit(solution)/shard_map/field/pallas_call | solution.py:276
  60.0 19.6 %all_to_all.15 = f32[64,1,128]{2,1,0:T(1,128)S(1)} all-to-all(f32[64,1,128]{2,1,0:T(1,128)} %bitcast.11), channel_id=1, replica_groups=mesh['gx'=8,'ya'=2,'yb'=2,'za'=8,'zb'=2] {'gx','ya','yb','zb'}, dimensions={0} | all-to-all | bytes 65536 | tf_op jit(solution)/shard_map/all_to_all | solution.py:295
  79.7 0.1 reduce_sum.18
  79.7 13.4 %all_to_all.16 = f32[8,1,128]{2,1,0:T(1,128)S(1)} all-to-all(f32[8,1,128]{2,1,0:T(1,128)S(1)} %broadcast_in_dim.2), channel_id=1, replica_groups=mesh['gx'=8,'ya'=2,'yb'=2,'za'=8,'zb'=2] {'za'}, dimensions={0} | all-to-all | bytes 8192 | tf_op jit(solution)/shard_map/all_to_all | solution.py:297
  93.1 0.7 div.6
  (5 shorter events, 0.0 us)
Async XLA Ops:
  17.2 8.0 %collective-permute-start = (s32[48,128]{1,0:T(8,128)}, s32[48,128]{1,0:T(8,128)S(1)}, u32[]{:S(2)}, u32[]{:S(2)}) collective-permute-start(s32[48,128]{1,0:T(8,128)} %get-tuple-element.12), channel_id=1, source_target_pairs={{0,64},{64,128},{128,192},{192,256},{256,320},{320,384},{384,448},... | collective-permute-start | bytes 73736 | tf_op jit(solution)/shard_map/ppermute | solution.py:228
  19.2 7.2 %collective-permute-start.1 = (s32[48,128]{1,0:T(8,128)}, s32[48,128]{1,0:T(8,128)S(1)}, u32[]{:S(2)}, u32[]{:S(2)}) collective-permute-start(s32[48,128]{1,0:T(8,128)} %get-tuple-element.13), channel_id=1, source_target_pairs={{0,448},{64,0},{128,64},{192,128},{256,192},{320,256},{384,320},{4... | collective-permute-start | bytes 73736 | tf_op jit(solution)/shard_map/ppermute | solution.py:228
  25.2 1.1 %copy-start = (s32[48,128]{1,0:T(8,128)}, s32[48,128]{1,0:T(8,128)S(1)}, u32[]{:S(2)}) copy-start(s32[48,128]{1,0:T(8,128)S(1)} %collective-permute-done.below) | copy-start | bytes 73732
  26.4 0.6 copy-start.1
  28.5 9.2 %collective-permute-start.2 = (s32[48,128]{1,0:T(8,128)}, s32[48,128]{1,0:T(8,128)S(1)}, u32[]{:S(2)}, u32[]{:S(2)}) collective-permute-start(s32[48,128]{1,0:T(8,128)} %get-tuple-element.14), channel_id=1, source_target_pairs={{0,1},{1,2},{2,3},{3,4},{4,5},{5,6},{6,7},{7,8},{8,9},{9,10},{10,1... | collective-permute-start | bytes 73736 | tf_op jit(solution)/shard_map/ppermute | solution.py:228
  32.8 6.3 %collective-permute-start.3 = (s32[48,128]{1,0:T(8,128)}, s32[48,128]{1,0:T(8,128)S(1)}, u32[]{:S(2)}, u32[]{:S(2)}) collective-permute-start(s32[48,128]{1,0:T(8,128)} %get-tuple-element.15), channel_id=1, source_target_pairs={{0,15},{1,0},{2,1},{3,2},{4,3},{5,4},{6,5},{7,6},{8,7},{9,8},{10,9... | collective-permute-start | bytes 73736 | tf_op jit(solution)/shard_map/ppermute | solution.py:228
  37.7 1.4 %copy-start.2 = (s32[48,128]{1,0:T(8,128)}, s32[48,128]{1,0:T(8,128)S(1)}, u32[]{:S(2)}) copy-start(s32[48,128]{1,0:T(8,128)S(1)} %collective-permute-done.2.under) | copy-start | bytes 73732
  39.1 0.6 copy-start.3

commit v2 on v1

--- a/solution.py
+++ b/solution.py
@@ -12,6 +12,7 @@
 LEVELS = 256
 NX, NW, NY = 4, 8, 128
 NZ = 4 * NW
+PITCH = NZ + 8
 GY = ("ya", "yb")
 GZ = ("za", "zb")
 NEAR = ("gx", "ya", "yb", "zb")
@@ -36,7 +37,9 @@
     return lax.broadcasted_iota(jnp.int32, shape, len(shape) - 1)
 
 
-def edge_kernel(bits, levels, out):
+def edge_kernel(bits, levels, out, bits_kept, levels_kept):
+    bits_kept[...] = bits[...]
+    levels_kept[...] = levels[...]
     lane = lanes((NW, NY))
     word = lax.broadcasted_iota(jnp.int32, (NW, NY), 0)
     mask = (lane // 16 == word) & (lane % 16 < 6)
@@ -48,10 +51,13 @@
             )
 
 
-def face_kernel(where, bits, levels, left, right, edges, low, high):
-    del where
+def face_kernel(bits, levels, gathered, edges, low, high):
+    count = gathered.shape[0] // NW
+    here = 2 * lax.axis_index("ya") + lax.axis_index("yb")
+    left = gathered[pl.ds(NW * ((here + count - 1) % count), NW), :]
+    right = gathered[pl.ds(NW * ((here + 1) % count), NW), :]
     lane = lanes((NW, NY))
-    both = jnp.where(lane % 16 < 3, left[...], right[...])
+    both = jnp.where(lane % 16 < 3, left, right)
     edges[...] = both
     for out, first in ((low, 0), (high, 1)):
         for i in range(3):
@@ -106,7 +112,7 @@
 def field_kernel(
     bits, levels, edges, below, above, under, over,
     previous, current, message,
-    strip, borders, v0, energy, v1, v2,
+    strip, borders, v0, energy, v1, v2, blocks, done,
 ):
     planes = plane_list(bits, levels, edges, below, above)
     strip[16:24] = jnp.zeros((8, NY), jnp.int32)
@@ -168,48 +174,47 @@
             result.append(energy[ex, ez, :, at] * (m, e)[half] - TWO * s)
         return result
 
-    UNROLL = 4
-    for x in range(8):
-
-        def first(i, carry, x=x):
-            for u in range(UNROLL):
-                z = i * UNROLL + u
-                for half, t in enumerate(step(v0, x + 1, z + 1, x, z)):
-                    v1[x, z, :, NY * half : NY * (half + 1)] = 0.5 * t
-            return carry
-
-        lax.fori_loop(0, (NZ + 4) // UNROLL, first, 0)
-
-    for x in range(6):
-
-        def second(i, carry, x=x):
-            for u in range(2):
-                z = i * 2 + u
-                for half, t in enumerate(step(v1, x + 1, z + 1, x + 1, z + 1)):
-                    at = slice(NY * half, NY * (half + 1))
-                    v2[x, z, :, at] = t - v0[x + 2, z + 2, :, at]
-            return carry
-
-        lax.fori_loop(0, (NZ + 2) // 2, second, 0)
-
-    sums = [jnp.zeros(tile, jnp.float32)] * 3
-    for x in range(NX):
-
-        def third(i, sums, x=x):
-            sums = list(sums)
-            for u in range(UNROLL):
-                z = i * UNROLL + u
-                t = step(v2, x + 1, z + 1, x + 2, z + 2, main_only=True)[0]
-                one = v1[x + 2, z + 2, :, :NY]
-                two = v2[x + 1, z + 1, :, :NY]
-                three = t - one
-                previous[pl.ds(x * NZ + z, PROBES, stride=NX * NZ), :] = two
-                current[pl.ds(x * NZ + z, PROBES, stride=NX * NZ), :] = three
-                sign = v0[x + 3, z + 3, :, :NY]
-                sums = [acc + sign * v for acc, v in zip(sums, (one, two, three))]
-            return tuple(sums)
-
-        sums = lax.fori_loop(0, NZ // UNROLL, third, tuple(sums))
+    def first(x, carry):
+        for z in range(NZ + 4):
+            for half, t in enumerate(step(v0, x + 1, z + 1, x, z)):
+                v1[x, z, :, NY * half : NY * (half + 1)] = 0.5 * t
+        return carry
+
+    lax.fori_loop(0, NX + 4, first, 0)
+
+    def second(x, carry):
+        for z in range(NZ + 2):
+            for half, t in enumerate(step(v1, x + 1, z + 1, x + 1, z + 1)):
+                at = slice(NY * half, NY * (half + 1))
+                v2[x, z, :, at] = t - v0[x + 2, z + 2, :, at]
+        return carry
+
+    lax.fori_loop(0, NX + 2, second, 0)
+
+    rows = blocks.reshape(2 * NX * PROBES * PITCH, NY)
+
+    def copy_out(n, x):
+        return pltpu.make_async_copy(
+            blocks.at[n, x, :, pl.ds(0, NZ), :], (previous, current)[n].at[:, x], done.at[n, x]
+        )
+
+    def third(x, sums):
+        sums = list(sums)
+        for z in range(NZ):
+            t = step(v2, x + 1, z + 1, x + 2, z + 2, main_only=True)[0]
+            one = v1[x + 2, z + 2, :, :NY]
+            two = v2[x + 1, z + 1, :, :NY]
+            three = t - one
+            for n, v in enumerate((two, three)):
+                at = (n * NX + x) * PROBES * PITCH + z
+                rows[pl.ds(at, PROBES, stride=PITCH), :] = v
+            sign = v0[x + 3, z + 3, :, :NY]
+            sums = [acc + sign * v for acc, v in zip(sums, (one, two, three))]
+        copy_out(0, x).start()
+        copy_out(1, x).start()
+        return tuple(sums)
+
+    sums = lax.fori_loop(0, NX, third, (jnp.zeros(tile, jnp.float32),) * 3)
 
     row = jnp.zeros(tile, jnp.float32)
     for n, acc in enumerate(sums):
@@ -217,10 +222,17 @@
         row = jnp.where(lane == 8 * n + probe, total, row)
     row = jnp.sum(row, axis=0, keepdims=True)
     message[...] = jnp.broadcast_to(row, message.shape)
-
-
-def shape(rows, dtype=jnp.int32):
-    return jax.ShapeDtypeStruct(rows, dtype)
+    for n in range(2):
+        for x in range(NX):
+            copy_out(n, x).wait()
+
+
+def local(rows, dtype=jnp.int32):
+    return pltpu.VMEM(rows, dtype)
+
+
+def keep(array):
+    return pltpu.with_memory_space_constraint(array, pltpu.VMEM)
 
 
 def shift(array, axis, by):
@@ -230,58 +242,52 @@
 
 def per_device(bits, levels):
     tile = (NW, NY)
-    edge = pl.pallas_call(
-        edge_kernel, out_shape=shape(tile), in_specs=vmem(2), out_specs=vmem(1)[0], name="edge"
+    edge, bits, levels = pl.pallas_call(
+        edge_kernel,
+        out_shape=(local(tile), local(bits.shape), local(levels.shape)),
+        in_specs=vmem(2),
+        out_specs=tuple(vmem(3)),
+        name="edge",
     )(bits, levels)
-    gathered = lax.all_gather(edge, GY)
-    count = lax.axis_size(GY)
-    here = lax.axis_index(GY)
-    where = jnp.stack([(here + count - 1) % count, (here + 1) % count]).astype(jnp.int32)
-    whole = pl.BlockSpec((NX, NW, NY), lambda i, w: (0, 0, 0))
-    flat = lambda rows: pl.BlockSpec((rows, NY), lambda i, w: (0, 0))
+    bits, levels = keep(bits), keep(levels)
+    gathered = keep(lax.all_gather(edge, GY, tiled=True))
     edges, low, high = pl.pallas_call(
         face_kernel,
-        out_shape=(shape(tile), shape((48, NY)), shape((48, NY))),
-        grid_spec=pltpu.PrefetchScalarGridSpec(
-            num_scalar_prefetch=1,
-            grid=(1,),
-            in_specs=[
-                whole,
-                whole,
-                pl.BlockSpec((None, NW, NY), lambda i, w: (w[0], 0, 0)),
-                pl.BlockSpec((None, NW, NY), lambda i, w: (w[1], 0, 0)),
-            ],
-            out_specs=[flat(NW), flat(48), flat(48)],
-        ),
+        out_shape=(local(tile), local((48, NY)), local((48, NY))),
+        in_specs=vmem(3),
+        out_specs=tuple(vmem(3)),
         name="face",
-    )(where, bits, levels, gathered, gathered)
-    below = shift(high, "gx", 1)
-    above = shift(low, "gx", -1)
+    )(bits, levels, gathered)
+    edges = keep(edges)
+    below = keep(shift(high, "gx", 1))
+    above = keep(shift(low, "gx", -1))
     z_low, z_high = pl.pallas_call(
         level_kernel,
-        out_shape=(shape((2 * ROWS, NY)),) * 2,
+        out_shape=(local((2 * ROWS, NY)),) * 2,
         in_specs=vmem(5),
         out_specs=tuple(vmem(2)),
         scratch_shapes=[pltpu.VMEM((ROWS, NY), jnp.int32)],
         name="level",
     )(bits, levels, edges, below, above)
-    under = shift(z_high, GZ, 1)
-    over = shift(z_low, GZ, -1)
+    under = keep(shift(z_high, GZ, 1))
+    over = keep(shift(z_low, GZ, -1))
     near = 1
     for axis in NEAR:
         near *= lax.axis_size(axis)
     far = lax.axis_size(FAR)
     total = near * far * NX * NZ * NY
     f32 = jnp.float32
+    block = (PROBES, NX, NZ, NY)
+    hbm = pl.BlockSpec(memory_space=pl.ANY)
     previous, current, message = pl.pallas_call(
         field_kernel,
         out_shape=(
-            shape((PROBES * NX * NZ, NY), f32),
-            shape((PROBES * NX * NZ, NY), f32),
-            shape((near, NY), f32),
+            jax.ShapeDtypeStruct(block, f32),
+            jax.ShapeDtypeStruct(block, f32),
+            local((near, NY), f32),
         ),
         in_specs=vmem(7),
-        out_specs=tuple(vmem(3)),
+        out_specs=(hbm, hbm, vmem(1)[0]),
         scratch_shapes=[
             pltpu.VMEM((ROWS, NY), jnp.int32),
             pltpu.VMEM((NW, ROWS, NY), jnp.int32),
@@ -289,6 +295,8 @@
             pltpu.VMEM((NX + 4, NZ + 4, PROBES, 2 * NY), f32),
             pltpu.VMEM((NX + 4, NZ + 4, PROBES, 2 * NY), f32),
             pltpu.VMEM((NX + 2, NZ + 2, PROBES, 2 * NY), f32),
+            pltpu.VMEM((2, NX, PROBES, PITCH, NY), f32),
+            pltpu.SemaphoreType.DMA((2, NX)),
         ],
         name="field",
     )(bits, levels, edges, below, above, under, over)
@@ -296,8 +304,7 @@
     spread = jnp.broadcast_to(part, (far, NY))
     summed = jnp.sum(lax.all_to_all(spread, FAR, 0, 0, tiled=True), axis=0)
     moments = summed[: 3 * PROBES].reshape(3, PROBES) / total
-    block = (PROBES, NX, NZ, NY)
-    return moments, previous.reshape(block), current.reshape(block)
+    return moments, previous, current
 
 
 def solution(mesh):

time: 94.5 us -> 72.2 us (0.76)
  Pallas kernels: 25.3 us -> 6.37 us
  local copies, waits for them, and re-layouts: 1.88 us -> 0.67 us
    pallas_call x4, Pallas kernels: 25.3 us -> 6.37 us  [the longest x1 5.46 us: per_device(): pl.pallas_call(field_kernel, out_shape=(jax.ShapeDtypeStruct(block, f32),...]
    unnamed x8 -> x0, local copies, waits for them, and re-layouts: 1.21 us -> none
where the time goes in v2:
time: 72.2 us; the launch traced here: 71.7 us
  blocking collectives  45 us (62%)
  starting transfers between devices  16.7 us (23%)
  Pallas kernels  6.37 us (9%)
  waiting for transfers between devices  2.15 us (3%)
    all_to_all x1, blocking collectives, per_device(): lax.all_to_all(message, NEAR, 0, 0, tiled=True)  19.8 us
    ppermute x4, starting transfers between devices, shift(): lax.ppermute(array, axis, [(i, (i + by) % count) for i in range(count)])  16.7 us
    all_to_all x1, blocking collectives, per_device(): summed = jnp.sum(lax.all_to_all(spread, FAR, 0, 0, tiled=True), axis=0)  13.4 us
    all_gather x1, blocking collectives, per_device(): gathered = keep(lax.all_gather(edge, GY, tiled=True))  11.9 us
    pallas_call x1, Pallas kernels, per_device(): pl.pallas_call(field_kernel, out_shape=(jax.ShapeDtypeStruct(block, f32),...  5.46 us
    ppermute x4, waiting for transfers between devices, shift(): lax.ppermute(array, axis, [(i, (i + by) % count) for i in range(count)])  2.15 us
  transfers between devices with their start and end apart: 4, of which 2 were waited for; matrix products, arithmetic and copies ran while one was open for 0% of the time, Pallas kernels for 0%

profile of v2, /device:TPU:1, one launch (start us, length us, event | category | flops | bytes accessed | tf_op | source)
XLA Modules:
  0.0 71.7 jit_solution(8264538424600622448)
XLA Ops:
  0.6 0.8 %edge.1 = (s32[8,128]{1,0:T(8,128)S(1)}, s32[4,8,128]{2,1,0:T(8,128)S(1)}, s32[4,8,128]{2,1,0:T(8,128)S(1)}) custom-call(s32[4,8,128]{2,1,0:T(8,128)} %bits.1, s32[4,8,128]{2,1,0:T(8,128)} %levels.1), custom_call_target="tpu_custom_call" | custom-call | tf_op jit(solution)/shard_map/edge/pallas_call | solution.py:245
  1.5 11.9 %all_gather.3.gathered = s32[32,128]{1,0:T(8,128)S(1)} all-gather(s32[8,128]{1,0:T(8,128)S(1)} %get-tuple-element.16), channel_id=1, replica_groups=mesh['gx'=8,'ya'=2,'yb'=2,'za'=8,'zb'=2] {'ya','yb'}, dimensions={0}, use_global_device_ids=true | all-gather | bytes 20480 | tf_op jit(solution)/shard_map/all_gather | solution.py:253
  13.3 1.9 %collective-permute-start = (s32[48,128]{1,0:T(8,128)S(1)}, s32[48,128]{1,0:T(8,128)S(1)}, u32[]{:S(2)}, u32[]{:S(2)}) collective-permute-start(s32[48,128]{1,0:T(8,128)S(1)} %get-tuple-element.18), channel_id=1, source_target_pairs={{0,64},{64,128},{128,192},{192,256},{256,320},{320,384},{384,448},... | collective-permute-start | bytes 73736 | tf_op jit(solution)/shard_map/ppermute | solution.py:240
  15.3 5.3 %collective-permute-start.1 = (s32[48,128]{1,0:T(8,128)S(1)}, s32[48,128]{1,0:T(8,128)S(1)}, u32[]{:S(2)}, u32[]{:S(2)}) collective-permute-start(s32[48,128]{1,0:T(8,128)S(1)} %get-tuple-element.19), channel_id=1, source_target_pairs={{0,448},{64,0},{128,64},{192,128},{256,192},{320,256},{384,320},{4... | collective-permute-start | bytes 73736 | tf_op jit(solution)/shard_map/ppermute | solution.py:240
  20.6 0.0 collective-permute-done.below
  20.6 0.9 %collective-permute-done.1.above = s32[48,128]{1,0:T(8,128)S(1)} collective-permute-done((s32[48,128]{1,0:T(8,128)S(1)}, s32[48,128]{1,0:T(8,128)S(1)}, u32[]{:S(2)}, u32[]{:S(2)}) %collective-permute-start.1) | collective-permute-done | bytes 24608 | tf_op jit(solution)/shard_map/ppermute | solution.py:240
  21.5 0.1 level.1
  21.6 4.6 %collective-permute-start.2 = (s32[48,128]{1,0:T(8,128)S(1)}, s32[48,128]{1,0:T(8,128)S(1)}, u32[]{:S(2)}, u32[]{:S(2)}) collective-permute-start(s32[48,128]{1,0:T(8,128)S(1)} %get-tuple-element.20), channel_id=1, source_target_pairs={{0,1},{1,2},{2,3},{3,4},{4,5},{5,6},{6,7},{7,8},{8,9},{9,10},{10,1... | collective-permute-start | bytes 73736 | tf_op jit(solution)/shard_map/ppermute | solution.py:240
  26.3 4.8 %collective-permute-start.3 = (s32[48,128]{1,0:T(8,128)S(1)}, s32[48,128]{1,0:T(8,128)S(1)}, u32[]{:S(2)}, u32[]{:S(2)}) collective-permute-start(s32[48,128]{1,0:T(8,128)S(1)} %get-tuple-element.21), channel_id=1, source_target_pairs={{0,15},{1,0},{2,1},{3,2},{4,3},{5,4},{6,5},{7,6},{8,7},{9,8},{10,9... | collective-permute-start | bytes 73736 | tf_op jit(solution)/shard_map/ppermute | solution.py:240
  31.1 0.0 collective-permute-done.2.under
  31.1 1.2 %collective-permute-done.3.over = s32[48,128]{1,0:T(8,128)S(1)} collective-permute-done((s32[48,128]{1,0:T(8,128)S(1)}, s32[48,128]{1,0:T(8,128)S(1)}, u32[]{:S(2)}, u32[]{:S(2)}) %collective-permute-start.3) | collective-permute-done | bytes 24608 | tf_op jit(solution)/shard_map/ppermute | solution.py:240
  32.3 5.5 %field.1 = (f32[8,4,32,128]{3,2,1,0:T(8,128)}, f32[8,4,32,128]{3,2,1,0:T(8,128)}, f32[64,128]{1,0:T(8,128)S(1)}) custom-call(s32[4,8,128]{2,1,0:T(8,128)S(1)} %get-tuple-element.14.bits, s32[4,8,128]{2,1,0:T(8,128)S(1)} %get-tuple-element.15.levels, s32[8,128]{1,0:T(8,128)S(1)} %get-tuple-element.17.edges, s32[48,128]{1,0:T(8,128)S(1)} %collective-permute-done.below, ...), custom_call_target="tpu_custom_call" | custom-call | tf_op jit(solution)/shard_map/field/pallas_call | solution.py:282
  37.8 19.8 %all_to_all.15 = f32[64,1,128]{2,1,0:T(1,128)S(1)} all-to-all(f32[64,1,128]{2,1,0:T(1,128)S(1)} %bitcast.4), channel_id=1, replica_groups=mesh['gx'=8,'ya'=2,'yb'=2,'za'=8,'zb'=2] {'gx','ya','yb','zb'}, dimensions={0} | all-to-all | bytes 65536 | tf_op jit(solution)/shard_map/all_to_all | solution.py:303
  57.5 0.1 reduce_sum.18
  57.6 13.4 %all_to_all.16 = f32[8,1,128]{2,1,0:T(1,128)S(1)} all-to-all(f32[8,1,128]{2,1,0:T(1,128)S(1)} %broadcast_in_dim.2), channel_id=1, replica_groups=mesh['gx'=8,'ya'=2,'yb'=2,'za'=8,'zb'=2] {'za'}, dimensions={0} | all-to-all | bytes 8192 | tf_op jit(solution)/shard_map/all_to_all | solution.py:305
  71.0 0.7 div.6
  (4 shorter events, 0.0 us)
Async XLA Ops:
  13.3 7.3 %collective-permute-start = (s32[48,128]{1,0:T(8,128)S(1)}, s32[48,128]{1,0:T(8,128)S(1)}, u32[]{:S(2)}, u32[]{:S(2)}) collective-permute-start(s32[48,128]{1,0:T(8,128)S(1)} %get-tuple-element.18), channel_id=1, source_target_pairs={{0,64},{64,128},{128,192},{192,256},{256,320},{320,384},{384,448},... | collective-permute-start | bytes 73736 | tf_op jit(solution)/shard_map/ppermute | solution.py:240
  15.3 6.3 %collective-permute-start.1 = (s32[48,128]{1,0:T(8,128)S(1)}, s32[48,128]{1,0:T(8,128)S(1)}, u32[]{:S(2)}, u32[]{:S(2)}) collective-permute-start(s32[48,128]{1,0:T(8,128)S(1)} %get-tuple-element.19), channel_id=1, source_target_pairs={{0,448},{64,0},{128,64},{192,128},{256,192},{320,256},{384,320},{4... | collective-permute-start | bytes 73736 | tf_op jit(solution)/shard_map/ppermute | solution.py:240
  21.6 9.5 %collective-permute-start.2 = (s32[48,128]{1,0:T(8,128)S(1)}, s32[48,128]{1,0:T(8,128)S(1)}, u32[]{:S(2)}, u32[]{:S(2)}) collective-permute-start(s32[48,128]{1,0:T(8,128)S(1)} %get-tuple-element.20), channel_id=1, source_target_pairs={{0,1},{1,2},{2,3},{3,4},{4,5},{5,6},{6,7},{7,8},{8,9},{9,10},{10,1... | collective-permute-start | bytes 73736 | tf_op jit(solution)/shard_map/ppermute | solution.py:240
  26.3 6.1 %collective-permute-start.3 = (s32[48,128]{1,0:T(8,128)S(1)}, s32[48,128]{1,0:T(8,128)S(1)}, u32[]{:S(2)}, u32[]{:S(2)}) collective-permute-start(s32[48,128]{1,0:T(8,128)S(1)} %get-tuple-element.21), channel_id=1, source_target_pairs={{0,15},{1,0},{2,1},{3,2},{4,3},{5,4},{6,5},{7,6},{8,7},{9,8},{10,9... | collective-permute-start | bytes 73736 | tf_op jit(solution)/shard_map/ppermute | solution.py:240

commit v3 on v0

v3 whole, which is shorter than its diff:
```python
import jax
import jax.numpy as jnp
from jax import lax
from jax.experimental import pallas as pl
from jax.experimental.pallas import tpu as pltpu
from jax.sharding import Mesh
from jax.sharding import PartitionSpec as P

PROBES = 8
LEVELS = 256
NX, NW, NY = 4, 8, 128
NZ = 4 * NW
PITCH = NZ + 8
GY = ("ya", "yb")
GZ = ("za", "zb")
REST = ("gx",) + GZ

disorder_width = 4.0
spectral_scale = 8.4
TWO = 2.0 / spectral_scale
E_MUL = TWO * disorder_width / LEVELS
E_ADD = TWO * disorder_width * (0.5 / LEVELS - 0.5)

PLANES = 18
ROWS = 24
FRACTION = 2.0**20


def vmem(n):
    return [pl.BlockSpec(memory_space=pltpu.VMEM)] * n


def lanes(shape):
    return lax.broadcasted_iota(jnp.int32, shape, len(shape) - 1)


def face_kernel(bits, levels, low, high, bits_kept, levels_kept):
    bits_kept[...] = bits[...]
    levels_kept[...] = levels[...]
    for out, first in ((low, 0), (high, 1)):
        for i in range(3):
            out[8 * i : 8 * i + 8] = bits[first + i]
        for i in range(2):
            out[24 + 8 * i : 32 + 8 * i] = levels[2 * first + i]


def plane_list(bits, levels, below, above):
    found = []
    for x in range(-3, 7):
        if x < 0:
            found.append((below, 8 * (x + 3)))
        elif x < NX:
            found.append((bits, x))
        else:
            found.append((above, 8 * (x - 4)))
    for x in range(-2, 6):
        if x < 0:
            found.append((below, 24 + 8 * (x + 2)))
        elif x < NX:
            found.append((levels, x))
        else:
            found.append((above, 24 + 8 * (x - 4)))
    return found


def plane_tile(plane):
    ref, at = plane
    if len(ref.shape) == 3:
        return ref[at]
    return ref[at : at + NW, :]


def word_row(plane, w):
    ref, at = plane
    if len(ref.shape) == 3:
        return ref[at, w : w + 1, :]
    return ref[at + w : at + w + 1, :]


def level_kernel(bits, levels, below, above, low, high):
    planes = plane_list(bits, levels, below, above)
    for out, w in ((low, 0), (high, NW - 1)):
        out[16:24] = jnp.zeros((8, NY), jnp.int32)
        for k, plane in enumerate(planes):
            out[k : k + 1] = word_row(plane, w)


def tiles():
    tile = (PROBES, NY)
    probe = lax.broadcasted_iota(jnp.int32, tile, 0)
    return tile, probe, lanes(tile), [jnp.left_shift(1, 4 * probe + j) for j in range(4)]


def sign_of(row, bit):
    return jnp.where((row & bit) != 0, 1.0, -1.0)


def energy_of(row, j):
    return (jnp.right_shift(row, 8 * j) & 255).astype(jnp.float32) * E_MUL + E_ADD


def step(v, energy, at, place):
    x, z = at
    own = v[x, z]
    s = pltpu.roll(own, NY - 1, 1) + pltpu.roll(own, 1, 1)
    s = s + (v[x + 1, z] + v[x - 1, z])
    s = s + (v[x, z + 1] + v[x, z - 1])
    return energy[place] * own - TWO * s


def sums_row(sums, mask, probe, lane):
    row = jnp.zeros(lane.shape, jnp.float32)
    for n, acc in enumerate(sums):
        total = jnp.sum(jnp.where(mask, acc, 0.0), axis=1, keepdims=True)
        row = jnp.where(lane == 8 * n + probe, total, row)
    return jnp.sum(row, axis=0, keepdims=True)


def main_kernel(
    bits, levels, below, above, under, over,
    strips, v2, v3,
    v0, energy, v1,
):
    planes = plane_list(bits, levels, below, above)
    tile, probe, lane, bit_of = tiles()

    word = lax.broadcasted_iota(jnp.int32, tile, 0)
    mask = (lane // 16 == word) & (lane % 16 < 12)
    strips[16:24] = jnp.zeros((8, NY), jnp.int32)
    for k, plane in enumerate(planes):
        rolled = pltpu.roll(plane_tile(plane), 6, 1, stride=16, stride_axis=0)
        strips[k : k + 1] = jnp.sum(jnp.where(mask, rolled, 0), axis=0, keepdims=True)
    wide = lanes((ROWS, NY))
    strips[ROWS:] = jnp.where(
        wide < 16, pltpu.roll(under[...], 6, 1), pltpu.roll(over[...], 6 + 112, 1)
    )

    def row_of(k, w):
        if w < 0:
            row = under[k : k + 1, :]
        elif w >= NW:
            row = over[k : k + 1, :]
        else:
            row = word_row(planes[k], w)
        return jnp.broadcast_to(row, tile)

    for w in range(-1, NW + 1):
        for k in range(10):
            row = row_of(k, w)
            for j in range(4):
                z = 4 * w + j
                if -3 <= z < NZ + 3:
                    v0[k, z + 3] = sign_of(row, bit_of[j])
        for k in range(8):
            row = row_of(10 + k, w)
            for j in range(4):
                z = 4 * w + j
                if -2 <= z < NZ + 2:
                    energy[k, z + 2] = energy_of(row, j)

    def first(i, carry):
        for u in range(2):
            x = 2 * i + u
            for z in range(NZ + 4):
                v1[x, z] = 0.5 * step(v0, energy, (x + 1, z + 1), (x, z))
        return carry

    lax.fori_loop(0, (NX + 4) // 2, first, 0)

    def second(i, carry):
        for u in range(2):
            x = 2 * i + u
            for z in range(NZ + 2):
                v2[x, z] = step(v1, energy, (x + 1, z + 1), (x + 1, z + 1)) - v0[x + 2, z + 2]
        return carry

    lax.fori_loop(0, (NX + 2) // 2, second, 0)

    def third(i, sums):
        sums = list(sums)
        for u in range(2):
            x = 2 * i + u
            for z in range(NZ):
                one = v1[x + 2, z + 2]
                two = v2[x + 1, z + 1]
                three = step(v2, energy, (x + 1, z + 1), (x + 2, z + 2)) - one
                v3[x, z] = three
                sign = v0[x + 3, z + 3]
                sums = [acc + sign * v for acc, v in zip(sums, (one, two, three))]
        return tuple(sums)

    sums = lax.fori_loop(0, NX // 2, third, (jnp.zeros(tile, jnp.float32),) * 3)
    row = sums_row(sums, (lane >= 3) & (lane < NY - 3), probe, lane)
    whole = row.astype(jnp.int32)
    part = (row - whole.astype(jnp.float32)) * FRACTION
    strips[PLANES : PLANES + 1] = whole
    strips[PLANES + 1 : PLANES + 2] = part.astype(jnp.int32)


def edge_kernel(
    gathered, v2, v3,
    previous, current, message,
    words, e0, energy, e1, e2, e3, blocks, done,
):
    count = gathered.shape[0] // (2 * ROWS)
    tile, probe, lane, bit_of = tiles()
    wide = lanes((ROWS, NY))

    def interfaces(i, sums):
        sums = list(sums)
        for u in range(2):
            k = 2 * i + u
            here, there = 2 * ROWS * k, 2 * ROWS * ((k + 1) % count)
            left = wide % 16 < 6
            own = jnp.where(left, gathered[pl.ds(here, ROWS), :], gathered[pl.ds(there, ROWS), :])
            far = jnp.where(
                left,
                gathered[pl.ds(here + ROWS, ROWS), :],
                gathered[pl.ds(there + ROWS, ROWS), :],
            )
            words[u, 0] = jnp.where(wide < 16, far, pltpu.roll(own, 16, 1))
            words[u, 1] = own
            words[u, 2] = jnp.where(wide >= 112, far, pltpu.roll(own, 112, 1))
        for u in range(2):
            for n in range(3):
                for k in range(10):
                    row = jnp.broadcast_to(words[u, n, k : k + 1, :], tile)
                    for j in range(4):
                        z = 4 * n - 4 + j
                        if -3 <= z < 7:
                            e0[u, k, z + 3] = sign_of(row, bit_of[j])
                for k in range(8):
                    row = jnp.broadcast_to(words[u, n, 10 + k : 11 + k, :], tile)
                    for j in range(4):
                        z = 4 * n - 4 + j
                        if -2 <= z < 6:
                            energy[u, k, z + 2] = energy_of(row, j)
        for u in range(2):
            for x in range(8):
                for z in range(8):
                    e1[u, x, z] = 0.5 * step(e0.at[u], energy.at[u], (x + 1, z + 1), (x, z))
        for u in range(2):
            for x in range(6):
                for z in range(6):
                    e2[2 * i + u, x, z] = (
                        step(e1.at[u], energy.at[u], (x + 1, z + 1), (x + 1, z + 1))
                        - e0[u, x + 2, z + 2]
                    )
        for u in range(2):
            for x in range(4):
                for z in range(4):
                    one = e1[u, x + 2, z + 2]
                    two = e2[2 * i + u, x + 1, z + 1]
                    three = (
                        step(e2.at[2 * i + u], energy.at[u], (x + 1, z + 1), (x + 2, z + 2)) - one
                    )
                    e3[2 * i + u, x, z] = three
                    sign = e0[u, x + 3, z + 3]
                    sums = [acc + sign * v for acc, v in zip(sums, (one, two, three))]
        return tuple(sums)

    sums = lax.fori_loop(0, count // 2, interfaces, (jnp.zeros(tile, jnp.float32),) * 3)

    here = 2 * lax.axis_index("ya") + lax.axis_index("yb")
    before = (here + count - 1) % count
    right = lane % 16 < 6
    outside = (lane < 3) | (lane >= NY - 3)
    rows = blocks.reshape(2 * NX * PROBES * PITCH, NY)

    def copy_out(n, x):
        return pltpu.make_async_copy(
            blocks.at[n, x, :, pl.ds(0, NZ), :], (previous, current)[n].at[:, x], done.at[n, x]
        )

    def merge(x, carry):
        for n, (main, edge, margin) in enumerate(((v2, e2, 1), (v3, e3, 0))):
            for j in range(4):
                fix = jnp.where(
                    right,
                    edge[here, x + margin, j + margin],
                    edge[before, x + margin, j + margin],
                )
                for w in range(NW):
                    z = 4 * w + j
                    moved = pltpu.roll(fix, (-16 * w - 6) % NY, 1)
                    value = jnp.where(outside, moved, main[x + margin, z + margin])
                    at = (n * NX + x) * PROBES * PITCH + z
                    rows[pl.ds(at, PROBES, stride=PITCH), :] = value
            copy_out(n, x).start()
        return carry

    lax.fori_loop(0, NX, merge, 0)

    row = sums_row(sums, (lane % 16 >= 3) & (lane % 16 < 9), probe, lane)
    for k in range(count):
        at = 2 * ROWS * k + PLANES
        whole = gathered[at : at + 1, :].astype(jnp.float32)
        part = gathered[at + 1 : at + 2, :].astype(jnp.float32)
        row = row + (whole + part * (1.0 / FRACTION))
    message[...] = jnp.broadcast_to(row, message.shape)
    for n in range(2):
        for x in range(NX):
            copy_out(n, x).wait()


def local(rows, dtype=jnp.int32):
    return pltpu.VMEM(rows, dtype)


def keep(array):
    return pltpu.with_memory_space_constraint(array, pltpu.VMEM)


def shift(array, axis, by):
    count = lax.axis_size(axis)
    return lax.ppermute(array, axis, [(i, (i + by) % count) for i in range(count)])


def per_device(bits, levels):
    f32 = jnp.float32
    low, high, bits, levels = pl.pallas_call(
        face_kernel,
        out_shape=(local((40, NY)), local((40, NY)), local(bits.shape), local(levels.shape)),
        in_specs=vmem(2),
        out_specs=tuple(vmem(4)),
        name="face",
    )(bits, levels)
    bits, levels = keep(bits), keep(levels)
    below = keep(shift(high, "gx", 1))
    above = keep(shift(low, "gx", -1))
    z_low, z_high = pl.pallas_call(
        level_kernel,
        out_shape=(local((ROWS, NY)),) * 2,
        in_specs=vmem(4),
        out_specs=tuple(vmem(2)),
        name="level",
    )(bits, levels, below, above)
    under = keep(shift(z_high, GZ, 1))
    over = keep(shift(z_low, GZ, -1))

    def field(margin, z_margin):
        return (NX + 2 * margin, NZ + 2 * z_margin, PROBES, NY)

    strips, v2, v3 = pl.pallas_call(
        main_kernel,
        out_shape=(
            local((2 * ROWS, NY)),
            local(field(1, 1), f32),
            local(field(0, 0), f32),
        ),
        in_specs=vmem(6),
        out_specs=tuple(vmem(3)),
        scratch_shapes=[
            pltpu.VMEM(field(3, 3), f32),
            pltpu.VMEM(field(2, 2), f32),
            pltpu.VMEM(field(2, 2), f32),
        ],
        name="main",
    )(bits, levels, below, above, under, over)
    gathered = keep(lax.all_gather(strips, GY, tiled=True))
    count = lax.axis_size(GY)
    rest = lax.axis_size(REST)
    total = rest * count * NX * NZ * NY
    block = (PROBES, NX, NZ, NY)
    hbm = pl.BlockSpec(memory_space=pl.ANY)

    def edge(n, margin):
        return pltpu.VMEM((n, 4 + 2 * margin, 4 + 2 * margin, PROBES, NY), f32)

    previous, current, message = pl.pallas_call(
        edge_kernel,
        out_shape=(
            jax.ShapeDtypeStruct(block, f32),
            jax.ShapeDtypeStruct(block, f32),
            local((rest, NY), f32),
        ),
        in_specs=vmem(3),
        out_specs=(hbm, hbm, vmem(1)[0]),
        scratch_shapes=[
            pltpu.VMEM((2, 3, ROWS, NY), jnp.int32),
            edge(2, 3),
            edge(2, 2),
            edge(2, 2),
            edge(count, 1),
            edge(count, 0),
            pltpu.VMEM((2, NX, PROBES, PITCH, NY), f32),
            pltpu.SemaphoreType.DMA((2, NX)),
        ],
        name="edges",
    )(gathered, keep(v2), keep(v3))
    summed = jnp.sum(lax.all_to_all(message, REST, 0, 0, tiled=True), axis=0)
    moments = summed[: 3 * PROBES].reshape(3, PROBES) / total
    return moments, previous, current


def solution(mesh):
    sizes = mesh.shape["gx"], mesh.shape["gy"], mesh.shape["gz"]
    torus = Mesh(
        mesh.devices.reshape(sizes[0], sizes[1] // 2, 2, sizes[2] // 2, 2),
        ("gx",) + GY + GZ,
    )
    return jax.shard_map(
        per_device,
        mesh=torus,
        in_specs=(P("gx", GZ, GY), P("gx", GZ, GY)),
        out_specs=(P(), P(None, "gx", GZ, GY), P(None, "gx", GZ, GY)),
        check_vma=False,
    )
```

time: 103 us -> 67.4 us (0.65)
  the two profiles are of different devices: /device:TPU:6 before, /device:TPU:1 now
where the time goes in v3:
time: 67.4 us; the launch traced here: 67 us
  blocking collectives  34.9 us (52%)
  starting transfers between devices  22.9 us (34%)
  Pallas kernels  5.68 us (8%)
  waiting for transfers between devices  2.02 us (3%)
  between operations  0.69 us (1%)
    all_to_all x1, blocking collectives, per_device(): summed = jnp.sum(lax.all_to_all(message, REST, 0, 0, tiled=True), axis=0)  26.9 us
    ppermute x4, starting transfers between devices, shift(): lax.ppermute(array, axis, [(i, (i + by) % count) for i in range(count)])  22.9 us
    all_gather x1, blocking collectives, per_device(): gathered = keep(lax.all_gather(strips, GY, tiled=True))  8.08 us
    pallas_call x1, Pallas kernels, per_device(): pl.pallas_call(edge_kernel, out_shape=(jax.ShapeDtypeStruct(block, f32),...  2.49 us
    pallas_call x1, Pallas kernels, per_device(): pl.pallas_call(main_kernel, out_shape=(local((2 * ROWS, NY)), local(field...  2.43 us
    ppermute x4, waiting for transfers between devices, shift(): lax.ppermute(array, axis, [(i, (i + by) % count) for i in range(count)])  2.02 us
  transfers between devices with their start and end apart: 4, of which 2 were waited for; matrix products, arithmetic and copies ran while one was open for 0% of the time, Pallas kernels for 0%

profile of v3, /device:TPU:1, one launch (start us, length us, event | category | flops | bytes accessed | tf_op | source)
XLA Modules:
  0.0 67.0 jit_solution(5740588825547872282)
XLA Ops:
  0.6 0.7 %face.1 = (s32[40,128]{1,0:T(8,128)S(1)}, s32[40,128]{1,0:T(8,128)S(1)}, s32[4,8,128]{2,1,0:T(8,128)S(1)}, s32[4,8,128]{2,1,0:T(8,128)S(1)}) custom-call(s32[4,8,128]{2,1,0:T(8,128)} %bits.1, s32[4,8,128]{2,1,0:T(8,128)} %levels.1), custom_call_target="tpu_custom_call" | custom-call | tf_op jit(solution)/shard_map/face/pallas_call | solution.py:321
  1.4 4.8 %collective-permute-start = (s32[40,128]{1,0:T(8,128)S(1)}, s32[40,128]{1,0:T(8,128)S(1)}, u32[]{:S(2)}, u32[]{:S(2)}) collective-permute-start(s32[40,128]{1,0:T(8,128)S(1)} %get-tuple-element.17), channel_id=1, source_target_pairs={{0,64},{64,128},{128,192},{192,256},{256,320},{320,384},{384,448},... | collective-permute-start | bytes 61448 | tf_op jit(solution)/shard_map/ppermute | solution.py:316
  6.2 8.6 %collective-permute-start.1 = (s32[40,128]{1,0:T(8,128)S(1)}, s32[40,128]{1,0:T(8,128)S(1)}, u32[]{:S(2)}, u32[]{:S(2)}) collective-permute-start(s32[40,128]{1,0:T(8,128)S(1)} %get-tuple-element.18), channel_id=1, source_target_pairs={{0,448},{64,0},{128,64},{192,128},{256,192},{320,256},{384,320},{4... | collective-permute-start | bytes 61448 | tf_op jit(solution)/shard_map/ppermute | solution.py:316
  14.8 0.0 collective-permute-done.below
  14.8 0.9 %collective-permute-done.1.above = s32[40,128]{1,0:T(8,128)S(1)} collective-permute-done((s32[40,128]{1,0:T(8,128)S(1)}, s32[40,128]{1,0:T(8,128)S(1)}, u32[]{:S(2)}, u32[]{:S(2)}) %collective-permute-start.1) | collective-permute-done | bytes 20512 | tf_op jit(solution)/shard_map/ppermute | solution.py:316
  15.7 4.7 %collective-permute-start.2 = (s32[24,128]{1,0:T(8,128)S(1)}, s32[24,128]{1,0:T(8,128)S(1)}, u32[]{:S(2)}, u32[]{:S(2)}) collective-permute-start(s32[24,128]{1,0:T(8,128)S(1)} %get-tuple-element.19), channel_id=1, source_target_pairs={{0,1},{1,2},{2,3},{3,4},{4,5},{5,6},{6,7},{7,8},{8,9},{9,10},{10,1... | collective-permute-start | bytes 36872 | tf_op jit(solution)/shard_map/ppermute | solution.py:316
  20.3 4.8 %collective-permute-start.3 = (s32[24,128]{1,0:T(8,128)S(1)}, s32[24,128]{1,0:T(8,128)S(1)}, u32[]{:S(2)}, u32[]{:S(2)}) collective-permute-start(s32[24,128]{1,0:T(8,128)S(1)} %get-tuple-element.20), channel_id=1, source_target_pairs={{0,15},{1,0},{2,1},{3,2},{4,3},{5,4},{6,5},{7,6},{8,7},{9,8},{10,9... | collective-permute-start | bytes 36872 | tf_op jit(solution)/shard_map/ppermute | solution.py:316
  25.2 0.0 collective-permute-done.2.under
  25.2 1.1 %collective-permute-done.3.over = s32[24,128]{1,0:T(8,128)S(1)} collective-permute-done((s32[24,128]{1,0:T(8,128)S(1)}, s32[24,128]{1,0:T(8,128)S(1)}, u32[]{:S(2)}, u32[]{:S(2)}) %collective-permute-start.3) | collective-permute-done | bytes 12320 | tf_op jit(solution)/shard_map/ppermute | solution.py:316
  26.3 2.4 %main.1 = (s32[48,128]{1,0:T(8,128)S(1)}, f32[6,34,8,128]{3,2,1,0:T(8,128)S(1)}, f32[4,32,8,128]{3,2,1,0:T(8,128)S(1)}) custom-call(s32[4,8,128]{2,1,0:T(8,128)S(1)} %get-tuple-element.15.bits, s32[4,8,128]{2,1,0:T(8,128)S(1)} %get-tuple-element.16.levels, s32[40,128]{1,0:T(8,128)S(1)} %collective-permute-done.below, ...), custom_call_target="tpu_custom_call" | custom-call | tf_op jit(solution)/shard_map/main/pallas_call | solution.py:344
  28.8 8.1 %all_gather.3.gathered = s32[192,128]{1,0:T(8,128)S(1)} all-gather(s32[48,128]{1,0:T(8,128)S(1)} %get-tuple-element.21), channel_id=1, replica_groups=mesh['gx'=8,'ya'=2,'yb'=2,'za'=8,'zb'=2] {'ya','yb'}, dimensions={0}, use_global_device_ids=true | all-gather | bytes 122880 | tf_op jit(solution)/shard_map/all_gather | solution.py:360
  36.8 2.5 %edges.1 = (f32[8,4,32,128]{3,2,1,0:T(8,128)}, f32[8,4,32,128]{3,2,1,0:T(8,128)}, f32[128,128]{1,0:T(8,128)S(1)}) custom-call(s32[192,128]{1,0:T(8,128)S(1)} %all_gather.3.gathered, f32[6,34,8,128]{3,2,1,0:T(8,128)S(1)} %get-tuple-element.22.v2, f32[4,32,8,128]{3,2,1,0:T(8,128)S(1)} %get-tuple-element.23.v3), custom_call_target="tpu_custom_call" | custom-call | tf_op jit(solution)/shard_map/edges/pallas_call | solution.py:370
  39.3 26.9 %all_to_all.9 = f32[128,1,128]{2,1,0:T(1,128)S(1)} all-to-all(f32[128,1,128]{2,1,0:T(1,128)S(1)} %bitcast.3), channel_id=1, replica_groups=mesh['gx'=8,'ya'=2,'yb'=2,'za'=8,'zb'=2] {'gx','za','zb'}, dimensions={0} | all-to-all | bytes 131072 | tf_op jit(solution)/shard_map/all_to_all | solution.py:391
  66.2 0.2 reduce_sum.9
  66.4 0.7 div.6
  (2 shorter events, 0.0 us)
Async XLA Ops:
  1.4 13.4 %collective-permute-start = (s32[40,128]{1,0:T(8,128)S(1)}, s32[40,128]{1,0:T(8,128)S(1)}, u32[]{:S(2)}, u32[]{:S(2)}) collective-permute-start(s32[40,128]{1,0:T(8,128)S(1)} %get-tuple-element.17), channel_id=1, source_target_pairs={{0,64},{64,128},{128,192},{192,256},{256,320},{320,384},{384,448},... | collective-permute-start | bytes 61448 | tf_op jit(solution)/shard_map/ppermute | solution.py:316
  6.2 9.5 %collective-permute-start.1 = (s32[40,128]{1,0:T(8,128)S(1)}, s32[40,128]{1,0:T(8,128)S(1)}, u32[]{:S(2)}, u32[]{:S(2)}) collective-permute-start(s32[40,128]{1,0:T(8,128)S(1)} %get-tuple-element.18), channel_id=1, source_target_pairs={{0,448},{64,0},{128,64},{192,128},{256,192},{320,256},{384,320},{4... | collective-permute-start | bytes 61448 | tf_op jit(solution)/shard_map/ppermute | solution.py:316
  15.7 9.5 %collective-permute-start.2 = (s32[24,128]{1,0:T(8,128)S(1)}, s32[24,128]{1,0:T(8,128)S(1)}, u32[]{:S(2)}, u32[]{:S(2)}) collective-permute-start(s32[24,128]{1,0:T(8,128)S(1)} %get-tuple-element.19), channel_id=1, source_target_pairs={{0,1},{1,2},{2,3},{3,4},{4,5},{5,6},{6,7},{7,8},{8,9},{9,10},{10,1... | collective-permute-start | bytes 36872 | tf_op jit(solution)/shard_map/ppermute | solution.py:316
  20.3 6.0 %collective-permute-start.3 = (s32[24,128]{1,0:T(8,128)S(1)}, s32[24,128]{1,0:T(8,128)S(1)}, u32[]{:S(2)}, u32[]{:S(2)}) collective-permute-start(s32[24,128]{1,0:T(8,128)S(1)} %get-tuple-element.20), channel_id=1, source_target_pairs={{0,15},{1,0},{2,1},{3,2},{4,3},{5,4},{6,5},{7,6},{8,7},{9,8},{10,9... | collective-permute-start | bytes 36872 | tf_op jit(solution)/shard_map/ppermute | solution.py:316

commit v4 on v3

--- a/solution.py
+++ b/solution.py
@@ -11,9 +11,10 @@
 NX, NW, NY = 4, 8, 128
 NZ = 4 * NW
 PITCH = NZ + 8
+GX = ("xa", "xb")
 GY = ("ya", "yb")
 GZ = ("za", "zb")
-REST = ("gx",) + GZ
+REST = GX + GZ
 
 disorder_width = 4.0
 spectral_scale = 8.4
@@ -24,6 +25,7 @@
 PLANES = 18
 ROWS = 24
 FRACTION = 2.0**20
+SMALL = pltpu.CompilerParams(vmem_limit_bytes=24 * 1024 * 1024)
 
 
 def vmem(n):
@@ -34,10 +36,17 @@
     return lax.broadcasted_iota(jnp.int32, shape, len(shape) - 1)
 
 
-def face_kernel(bits, levels, low, high, bits_kept, levels_kept):
-    bits_kept[...] = bits[...]
-    levels_kept[...] = levels[...]
-    for out, first in ((low, 0), (high, 1)):
+def face_kernel(bits_far, levels_far, even, odd, bits, levels, done):
+    copies = [
+        pltpu.make_async_copy(bits_far, bits, done.at[0]),
+        pltpu.make_async_copy(levels_far, levels, done.at[1]),
+    ]
+    for copy in copies:
+        copy.start()
+    for copy in copies:
+        copy.wait()
+    upper = lax.axis_index("xb")
+    for out, first in ((even, 1 - upper), (odd, upper)):
         for i in range(3):
             out[8 * i : 8 * i + 8] = bits[first + i]
         for i in range(2):
@@ -77,7 +86,11 @@
     return ref[at + w : at + w + 1, :]
 
 
-def level_kernel(bits, levels, below, above, low, high):
+def level_kernel(bits, levels, even, odd, below, above, low, high):
+    upper = lax.axis_index("xb")
+    near, far = even[pl.ds(40 * (1 - upper), 40), :], odd[...]
+    below[...] = jnp.where(upper == 1, near, far)
+    above[...] = jnp.where(upper == 1, far, near)
     planes = plane_list(bits, levels, below, above)
     for out, w in ((low, 0), (high, NW - 1)):
         out[16:24] = jnp.zeros((8, NY), jnp.int32)
@@ -116,80 +129,101 @@
     return jnp.sum(row, axis=0, keepdims=True)
 
 
-def main_kernel(
-    bits, levels, below, above, under, over,
-    strips, v2, v3,
-    v0, energy, v1,
-):
+def add_sums(sums, v0, x, z, values):
+    sign = v0[x + 3, z + 3]
+    return [acc + sign * v for acc, v in zip(sums, values)]
+
+
+def inner_kernel(bits, levels, below, above, strips, sums_out, v0, energy, v1, v2, v3):
     planes = plane_list(bits, levels, below, above)
     tile, probe, lane, bit_of = tiles()
-
     word = lax.broadcasted_iota(jnp.int32, tile, 0)
     mask = (lane // 16 == word) & (lane % 16 < 12)
     strips[16:24] = jnp.zeros((8, NY), jnp.int32)
     for k, plane in enumerate(planes):
         rolled = pltpu.roll(plane_tile(plane), 6, 1, stride=16, stride_axis=0)
         strips[k : k + 1] = jnp.sum(jnp.where(mask, rolled, 0), axis=0, keepdims=True)
+
+    for w in range(NW):
+        for k in range(10):
+            row = jnp.broadcast_to(word_row(planes[k], w), tile)
+            for j in range(4):
+                v0[k, 4 * w + j + 3] = sign_of(row, bit_of[j])
+        for k in range(8):
+            row = jnp.broadcast_to(word_row(planes[10 + k], w), tile)
+            for j in range(4):
+                energy[k, 4 * w + j + 2] = energy_of(row, j)
+
+    def first(i, carry):
+        for u in range(2):
+            x = 2 * i + u
+            for z in range(3, NZ + 1):
+                v1[x, z] = 0.5 * step(v0, energy, (x + 1, z + 1), (x, z))
+        return carry
+
+    lax.fori_loop(0, (NX + 4) // 2, first, 0)
+
+    def second(i, carry):
+        for u in range(2):
+            x = 2 * i + u
+            for z in range(3, NZ - 1):
+                v2[x, z] = step(v1, energy, (x + 1, z + 1), (x + 1, z + 1)) - v0[x + 2, z + 2]
+        return carry
+
+    lax.fori_loop(0, (NX + 2) // 2, second, 0)
+
+    def third(i, sums):
+        for u in range(2):
+            x = 2 * i + u
+            for z in range(3, NZ - 3):
+                one = v1[x + 2, z + 2]
+                two = v2[x + 1, z + 1]
+                three = step(v2, energy, (x + 1, z + 1), (x + 2, z + 2)) - one
+                v3[x, z] = three
+                sums = add_sums(sums, v0, x, z, (one, two, three))
+        return tuple(sums)
+
+    sums = lax.fori_loop(0, NX // 2, third, (jnp.zeros(tile, jnp.float32),) * 3)
+    for n in range(3):
+        sums_out[n] = sums[n]
+
+
+def outer_kernel(
+    under, over, strips_in, sums_in, v0_in, energy_in, v1_in, v2_in, v3_in,
+    strips, v0, energy, v1, v2, v3,
+):
+    del v0_in, energy_in, v1_in, v2_in, v3_in
+    tile, probe, lane, bit_of = tiles()
+    strips[:ROWS] = strips_in[...]
     wide = lanes((ROWS, NY))
     strips[ROWS:] = jnp.where(
         wide < 16, pltpu.roll(under[...], 6, 1), pltpu.roll(over[...], 6 + 112, 1)
     )
-
-    def row_of(k, w):
-        if w < 0:
-            row = under[k : k + 1, :]
-        elif w >= NW:
-            row = over[k : k + 1, :]
-        else:
-            row = word_row(planes[k], w)
-        return jnp.broadcast_to(row, tile)
-
-    for w in range(-1, NW + 1):
+    for ref, base in ((under, -4), (over, NZ)):
         for k in range(10):
-            row = row_of(k, w)
+            row = jnp.broadcast_to(ref[k : k + 1, :], tile)
             for j in range(4):
-                z = 4 * w + j
-                if -3 <= z < NZ + 3:
-                    v0[k, z + 3] = sign_of(row, bit_of[j])
+                if -3 <= base + j < NZ + 3:
+                    v0[k, base + j + 3] = sign_of(row, bit_of[j])
         for k in range(8):
-            row = row_of(10 + k, w)
+            row = jnp.broadcast_to(ref[10 + k : 11 + k, :], tile)
             for j in range(4):
-                z = 4 * w + j
-                if -2 <= z < NZ + 2:
-                    energy[k, z + 2] = energy_of(row, j)
-
-    def first(i, carry):
-        for u in range(2):
-            x = 2 * i + u
-            for z in range(NZ + 4):
-                v1[x, z] = 0.5 * step(v0, energy, (x + 1, z + 1), (x, z))
-        return carry
-
-    lax.fori_loop(0, (NX + 4) // 2, first, 0)
-
-    def second(i, carry):
-        for u in range(2):
-            x = 2 * i + u
-            for z in range(NZ + 2):
-                v2[x, z] = step(v1, energy, (x + 1, z + 1), (x + 1, z + 1)) - v0[x + 2, z + 2]
-        return carry
-
-    lax.fori_loop(0, (NX + 2) // 2, second, 0)
-
-    def third(i, sums):
-        sums = list(sums)
-        for u in range(2):
-            x = 2 * i + u
-            for z in range(NZ):
-                one = v1[x + 2, z + 2]
-                two = v2[x + 1, z + 1]
-                three = step(v2, energy, (x + 1, z + 1), (x + 2, z + 2)) - one
-                v3[x, z] = three
-                sign = v0[x + 3, z + 3]
-                sums = [acc + sign * v for acc, v in zip(sums, (one, two, three))]
-        return tuple(sums)
-
-    sums = lax.fori_loop(0, NX // 2, third, (jnp.zeros(tile, jnp.float32),) * 3)
+                if -2 <= base + j < NZ + 2:
+                    energy[k, base + j + 2] = energy_of(row, j)
+    for x in range(NX + 4):
+        for z in (0, 1, 2, NZ + 1, NZ + 2, NZ + 3):
+            v1[x, z] = 0.5 * step(v0, energy, (x + 1, z + 1), (x, z))
+    for x in range(NX + 2):
+        for z in (0, 1, 2, NZ - 1, NZ, NZ + 1):
+            v2[x, z] = step(v1, energy, (x + 1, z + 1), (x + 1, z + 1)) - v0[x + 2, z + 2]
+    sums = [sums_in[n] for n in range(3)]
+    for x in range(NX):
+        for z in (0, 1, 2, NZ - 3, NZ - 2, NZ - 1):
+            one = v1[x + 2, z + 2]
+            two = v2[x + 1, z + 1]
+            three = step(v2, energy, (x + 1, z + 1), (x + 2, z + 2)) - one
+            v3[x, z] = three
+            sums = add_sums(sums, v0, x, z, (one, two, three))
     row = sums_row(sums, (lane >= 3) & (lane < NY - 3), probe, lane)
     whole = row.astype(jnp.int32)
     part = (row - whole.astype(jnp.float32)) * FRACTION
@@ -318,45 +352,54 @@
 
 def per_device(bits, levels):
     f32 = jnp.float32
-    low, high, bits, levels = pl.pallas_call(
+    face = (40, NY)
+    even, odd, bits, levels = pl.pallas_call(
         face_kernel,
-        out_shape=(local((40, NY)), local((40, NY)), local(bits.shape), local(levels.shape)),
-        in_specs=vmem(2),
+        out_shape=(local(face), local(face), local(bits.shape), local(levels.shape)),
+        in_specs=[pl.BlockSpec(memory_space=pltpu.HBM)] * 2,
         out_specs=tuple(vmem(4)),
+        scratch_shapes=[pltpu.SemaphoreType.DMA((2,))],
         name="face",
+        compiler_params=SMALL,
     )(bits, levels)
     bits, levels = keep(bits), keep(levels)
-    below = keep(shift(high, "gx", 1))
-    above = keep(shift(low, "gx", -1))
-    z_low, z_high = pl.pallas_call(
+    size = lax.axis_size(GX)
+    across = [(i, (i + 1) % size if i % 2 else (i - 1) % size) for i in range(size)]
+    odd = keep(lax.ppermute(odd, GX, across))
+    even = keep(lax.all_gather(even, "xb", tiled=True))
+    below, above, z_low, z_high = pl.pallas_call(
         level_kernel,
-        out_shape=(local((ROWS, NY)),) * 2,
+        out_shape=(local(face),) * 2 + (local((ROWS, NY)),) * 2,
         in_specs=vmem(4),
-        out_specs=tuple(vmem(2)),
+        out_specs=tuple(vmem(4)),
         name="level",
-    )(bits, levels, below, above)
+        compiler_params=SMALL,
+    )(bits, levels, even, odd)
     under = keep(shift(z_high, GZ, 1))
     over = keep(shift(z_low, GZ, -1))
 
-    def field(margin, z_margin):
-        return (NX + 2 * margin, NZ + 2 * z_margin, PROBES, NY)
-
-    strips, v2, v3 = pl.pallas_call(
-        main_kernel,
-        out_shape=(
-            local((2 * ROWS, NY)),
-            local(field(1, 1), f32),
-            local(field(0, 0), f32),
-        ),
-        in_specs=vmem(6),
-        out_specs=tuple(vmem(3)),
-        scratch_shapes=[
-            pltpu.VMEM(field(3, 3), f32),
-            pltpu.VMEM(field(2, 2), f32),
-            pltpu.VMEM(field(2, 2), f32),
-        ],
-        name="main",
-    )(bits, levels, below, above, under, over)
+    def field(margin):
+        return local((NX + 2 * margin, NZ + 2 * margin, PROBES, NY), f32)
+
+    fields = [field(margin) for margin in (3, 2, 2, 1, 0)]
+    strips, *inner = pl.pallas_call(
+        inner_kernel,
+        out_shape=(local((ROWS, NY)), local((3, PROBES, NY), f32), *fields),
+        in_specs=vmem(4),
+        out_specs=tuple(vmem(7)),
+        name="inner",
+        compiler_params=SMALL,
+    )(bits, levels, keep(below), keep(above))
+    inner = [keep(array) for array in (strips, *inner)]
+    strips, *_, v2, v3 = pl.pallas_call(
+        outer_kernel,
+        out_shape=(local((2 * ROWS, NY)), *fields),
+        in_specs=vmem(9),
+        out_specs=tuple(vmem(6)),
+        input_output_aliases={4 + i: 1 + i for i in range(5)},
+        name="outer",
+        compiler_params=SMALL,
+    )(under, over, *inner)
     gathered = keep(lax.all_gather(strips, GY, tiled=True))
     count = lax.axis_size(GY)
     rest = lax.axis_size(REST)
@@ -387,6 +430,7 @@
             pltpu.SemaphoreType.DMA((2, NX)),
         ],
         name="edges",
+        compiler_params=SMALL,
     )(gathered, keep(v2), keep(v3))
     summed = jnp.sum(lax.all_to_all(message, REST, 0, 0, tiled=True), axis=0)
     moments = summed[: 3 * PROBES].reshape(3, PROBES) / total
@@ -394,15 +438,12 @@
 
 
 def solution(mesh):
-    sizes = mesh.shape["gx"], mesh.shape["gy"], mesh.shape["gz"]
-    torus = Mesh(
-        mesh.devices.reshape(sizes[0], sizes[1] // 2, 2, sizes[2] // 2, 2),
-        ("gx",) + GY + GZ,
-    )
+    halves = [n for axis in ("gx", "gy", "gz") for n in (mesh.shape[axis] // 2, 2)]
+    torus = Mesh(mesh.devices.reshape(halves), GX + GY + GZ)
     return jax.shard_map(
         per_device,
         mesh=torus,
-        in_specs=(P("gx", GZ, GY), P("gx", GZ, GY)),
-        out_specs=(P(), P(None, "gx", GZ, GY), P(None, "gx", GZ, GY)),
+        in_specs=(P(GX, GZ, GY), P(GX, GZ, GY)),
+        out_specs=(P(), P(None, GX, GZ, GY), P(None, GX, GZ, GY)),
         check_vma=False,
     )

time: 67.4 us -> 64.6 us (0.958)
  waiting for transfers between devices: 2.02 us -> 0.01 us
  starting transfers between devices: 22.9 us -> 21 us
  local copies, waits for them, and re-layouts: 0.66 us -> 2.09 us
    ppermute x4 -> x2, starting transfers between devices: 22.9 us -> 9.48 us  [shift(): lax.ppermute(array, axis, [(i, (i + by) % count) for i in range(count)])]
    ppermute x0 -> x1, starting transfers between devices: none -> 11.5 us  [per_device(): odd = keep(lax.ppermute(odd, GX, across))]
    all_gather x0 -> x1, blocking collectives: none -> 3.3 us  [per_device(): even = keep(lax.all_gather(even, 'xb', tiled=True))]
    all_to_all x1, blocking collectives: 26.9 us -> 24.3 us  [per_device(): summed = jnp.sum(lax.all_to_all(message, REST, 0, 0, tiled=True), axis=0)]
    ppermute x4 -> x2, waiting for transfers between devices: 2.02 us -> 0.01 us  [shift(): lax.ppermute(array, axis, [(i, (i + by) % count) for i in range(count)])]
    unnamed x0 -> x4, local copies, waits for them, and re-layouts: none -> 1.43 us
    pallas_call x3 -> x4, Pallas kernels: 3.19 us -> 2.53 us  [the longest x1 2.07 us: per_device(): pl.pallas_call(inner_kernel, out_shape=(local((ROWS, NY)), local((3, PROB...]
  transfers between devices with their start and end apart: 4 -> 3, of which waited for: 2 -> 0; matrix products, arithmetic and copies ran while one was open for 0% -> 0% of each run, Pallas kernels for 0% -> 3%
where the time goes in v4:
time: 64.6 us; the launch traced here: 64.3 us
  blocking collectives  35.3 us (55%)
  starting transfers between devices  21 us (33%)
  Pallas kernels  5.02 us (8%)
  local copies, waits for them, and re-layouts  2.09 us (3%)
  between operations  0.72 us (1%)
    all_to_all x1, blocking collectives, per_device(): summed = jnp.sum(lax.all_to_all(message, REST, 0, 0, tiled=True), axis=0)  24.3 us
    ppermute x1, starting transfers between devices, per_device(): odd = keep(lax.ppermute(odd, GX, across))  11.5 us
    ppermute x2, starting transfers between devices, shift(): lax.ppermute(array, axis, [(i, (i + by) % count) for i in range(count)])  9.48 us
    all_gather x1, blocking collectives, per_device(): gathered = keep(lax.all_gather(strips, GY, tiled=True))  7.71 us
    all_gather x1, blocking collectives, per_device(): even = keep(lax.all_gather(even, 'xb', tiled=True))  3.3 us
    pallas_call x1, Pallas kernels, per_device(): pl.pallas_call(edge_kernel, out_shape=(jax.ShapeDtypeStruct(block, f32),...  2.49 us
    pallas_call x1, Pallas kernels, per_device(): pl.pallas_call(inner_kernel, out_shape=(local((ROWS, NY)), local((3, PROB...  2.07 us
    unnamed x4, local copies, waits for them, and re-layouts  1.43 us
  transfers between devices with their start and end apart: 3, of which 0 were waited for; matrix products, arithmetic and copies ran while one was open for 0% of the time, Pallas kernels for 3%

profile of v4, /device:TPU:1, one launch (start us, length us, event | category | flops | bytes accessed | tf_op | source)
XLA Modules:
  0.0 64.3 jit_solution(13754252060056550826)
XLA Ops:
  0.6 0.0 copy-start
  0.6 0.7 %copy-done = s32[4,8,128]{2,1,0:T(8,128)S(1)} copy-done((s32[4,8,128]{2,1,0:T(8,128)S(1)}, s32[4,8,128]{2,1,0:T(8,128)}, u32[]{:S(2)}) %copy-start) | copy-done | bytes 16408
  1.3 0.0 copy-start.1
  1.4 0.7 %copy-done.1 = s32[4,8,128]{2,1,0:T(8,128)S(1)} copy-done((s32[4,8,128]{2,1,0:T(8,128)S(1)}, s32[4,8,128]{2,1,0:T(8,128)}, u32[]{:S(2)}) %copy-start.1) | copy-done | bytes 16408
  2.1 11.5 %collective-permute-start = (s32[40,128]{1,0:T(8,128)S(1)}, s32[40,128]{1,0:T(8,128)S(1)}, u32[]{:S(2)}, u32[]{:S(2)}) collective-permute-start(s32[40,128]{1,0:T(8,128)S(1)} %get-tuple-element.27), channel_id=1, source_target_pairs={{0,448},{64,128},{128,64},{192,256},{256,192},{320,384},{384,320},... | collective-permute-start | bytes 61448 | tf_op jit(solution)/shard_map/ppermute | solution.py:368
  13.6 3.3 %all_gather.6.even = s32[80,128]{1,0:T(8,128)S(1)} all-gather(s32[40,128]{1,0:T(8,128)S(1)} %get-tuple-element.26), channel_id=1, replica_groups=mesh['xa'=4,'xb'=2,'ya'=2,'yb'=2,'za'=8,'zb'=2] {'xb'}, dimensions={0}, use_global_device_ids=true | all-gather | bytes 61440 | tf_op jit(solution)/shard_map/all_gather | solution.py:369
  16.9 0.0 collective-permute-done.odd
  16.9 4.7 %collective-permute-start.1 = (s32[24,128]{1,0:T(8,128)S(1)}, s32[24,128]{1,0:T(8,128)S(1)}, u32[]{:S(2)}, u32[]{:S(2)}) collective-permute-start(s32[24,128]{1,0:T(8,128)S(1)} %get-tuple-element.28), channel_id=1, source_target_pairs={{0,1},{1,2},{2,3},{3,4},{4,5},{5,6},{6,7},{7,8},{8,9},{9,10},{10,1... | collective-permute-start | bytes 36872 | tf_op jit(solution)/shard_map/ppermute | solution.py:350
  21.6 4.8 %collective-permute-start.2 = (s32[24,128]{1,0:T(8,128)S(1)}, s32[24,128]{1,0:T(8,128)S(1)}, u32[]{:S(2)}, u32[]{:S(2)}) collective-permute-start(s32[24,128]{1,0:T(8,128)S(1)} %get-tuple-element.29), channel_id=1, source_target_pairs={{0,15},{1,0},{2,1},{3,2},{4,3},{5,4},{6,5},{7,6},{8,7},{9,8},{10,9... | collective-permute-start | bytes 36872 | tf_op jit(solution)/shard_map/ppermute | solution.py:350
  26.4 2.1 %inner.1 = (s32[24,128]{1,0:T(8,128)S(1)}, f32[3,8,128]{2,1,0:T(8,128)S(1)}, f32[10,38,8,128]{3,2,1,0:T(8,128)S(1)}, f32[8,36,8,128]{3,2,1,0:T(8,128)S(1)}, f32[...) custom-call(s32[4,8,128]{2,1,0:T(8,128)S(1)} %get-tuple-element.24.bits, ...), custom_call_target="tpu_custom_call" | custom-call | tf_op jit(solution)/shard_map/inner/pallas_call | solution.py:385
  28.5 0.0 collective-permute-done.1.under
  28.5 0.0 collective-permute-done.2.over
  28.5 0.4 outer.1
  28.9 7.7 %all_gather.7.gathered = s32[192,128]{1,0:T(8,128)S(1)} all-gather(s32[48,128]{1,0:T(8,128)S(1)} %get-tuple-element.39), channel_id=1, replica_groups=mesh['xa'=4,'xb'=2,'ya'=2,'yb'=2,'za'=8,'zb'=2] {'ya','yb'}, dimensions={0}, use_global_device_ids=true | all-gather | bytes 122880 | tf_op jit(solution)/shard_map/all_gather | solution.py:403
  36.6 2.5 %edges.1 = (f32[8,4,32,128]{3,2,1,0:T(8,128)}, f32[8,4,32,128]{3,2,1,0:T(8,128)}, f32[128,128]{1,0:T(8,128)S(1)}) custom-call(s32[192,128]{1,0:T(8,128)S(1)} %all_gather.7.gathered, f32[6,34,8,128]{3,2,1,0:T(8,128)S(1)} %get-tuple-element.40.v2, f32[4,32,8,128]{3,2,1,0:T(8,128)S(1)} %get-tuple-element.41.v3), custom_call_target="tpu_custom_call" | custom-call | tf_op jit(solution)/shard_map/edges/pallas_call | solution.py:413
  39.1 24.3 %all_to_all.9 = f32[128,1,128]{2,1,0:T(1,128)S(1)} all-to-all(f32[128,1,128]{2,1,0:T(1,128)S(1)} %bitcast.3), channel_id=1, replica_groups=mesh['xa'=4,'xb'=2,'ya'=2,'yb'=2,'za'=8,'zb'=2] {'xa','xb','za','zb'}, dimensions={0} | all-to-all | bytes 131072 | tf_op jit(solution)/shard_map/all_to_all | solution.py:435
  63.4 0.2 reduce_sum.9
  63.6 0.7 %div.6 = f32[3,8]{1,0:T(4,128)} reshape(f32[24]{0:T(128)S(1)} %slice_multiply_fusion) | data formatting | bytes 192 | tf_op jit(solution)/shard_map/div | solution.py:436
  (3 shorter events, 0.1 us)
Async XLA Ops:
  0.6 0.7 %copy-start = (s32[4,8,128]{2,1,0:T(8,128)S(1)}, s32[4,8,128]{2,1,0:T(8,128)}, u32[]{:S(2)}) copy-start(s32[4,8,128]{2,1,0:T(8,128)} %bits_far.1) | copy-start | bytes 49156
  1.3 0.7 %copy-start.1 = (s32[4,8,128]{2,1,0:T(8,128)S(1)}, s32[4,8,128]{2,1,0:T(8,128)}, u32[]{:S(2)}) copy-start(s32[4,8,128]{2,1,0:T(8,128)} %levels_far.1) | copy-start | bytes 49156
  2.1 14.8 %collective-permute-start = (s32[40,128]{1,0:T(8,128)S(1)}, s32[40,128]{1,0:T(8,128)S(1)}, u32[]{:S(2)}, u32[]{:S(2)}) collective-permute-start(s32[40,128]{1,0:T(8,128)S(1)} %get-tuple-element.27), channel_id=1, source_target_pairs={{0,448},{64,128},{128,64},{192,256},{256,192},{320,384},{384,320},... | collective-permute-start | bytes 61448 | tf_op jit(solution)/shard_map/ppermute | solution.py:368
  16.9 11.6 %collective-permute-start.1 = (s32[24,128]{1,0:T(8,128)S(1)}, s32[24,128]{1,0:T(8,128)S(1)}, u32[]{:S(2)}, u32[]{:S(2)}) collective-permute-start(s32[24,128]{1,0:T(8,128)S(1)} %get-tuple-element.28), channel_id=1, source_target_pairs={{0,1},{1,2},{2,3},{3,4},{4,5},{5,6},{6,7},{7,8},{8,9},{9,10},{10,1... | collective-permute-start | bytes 36872 | tf_op jit(solution)/shard_map/ppermute | solution.py:350
  21.6 6.9 %collective-permute-start.2 = (s32[24,128]{1,0:T(8,128)S(1)}, s32[24,128]{1,0:T(8,128)S(1)}, u32[]{:S(2)}, u32[]{:S(2)}) collective-permute-start(s32[24,128]{1,0:T(8,128)S(1)} %get-tuple-element.29), channel_id=1, source_target_pairs={{0,15},{1,0},{2,1},{3,2},{4,3},{5,4},{6,5},{7,6},{8,7},{9,8},{10,9... | collective-permute-start | bytes 36872 | tf_op jit(solution)/shard_map/ppermute | solution.py:350

commit v5 on v4

--- a/solution.py
+++ b/solution.py
@@ -1,3 +1,6 @@
+import functools
+import itertools
+
 import jax
 import jax.numpy as jnp
 from jax import lax
@@ -15,6 +18,7 @@
 GY = ("ya", "yb")
 GZ = ("za", "zb")
 REST = GX + GZ
+EVERY = GX + GY + GZ
 
 disorder_width = 4.0
 spectral_scale = 8.4
@@ -234,16 +238,18 @@
 def edge_kernel(
     gathered, v2, v3,
     previous, current, message,
-    words, e0, energy, e1, e2, e3, blocks, done,
+    words, e0, energy, e1, e2, e3, partial, blocks, done,
 ):
     count = gathered.shape[0] // (2 * ROWS)
     tile, probe, lane, bit_of = tiles()
     wide = lanes((ROWS, NY))
 
-    def interfaces(i, sums):
-        sums = list(sums)
-        for u in range(2):
-            k = 2 * i + u
+    place = 2 * lax.axis_index("ya") + lax.axis_index("yb")
+    first = place + count - 1
+
+    def interfaces(i, carry):
+        for u in range(2):
+            k = (first + 2 * i + u) % count
             here, there = 2 * ROWS * k, 2 * ROWS * ((k + 1) % count)
             left = wide % 16 < 6
             own = jnp.where(left, gathered[pl.ds(here, ROWS), :], gathered[pl.ds(there, ROWS), :])
@@ -281,6 +287,7 @@
                         - e0[u, x + 2, z + 2]
                     )
         for u in range(2):
+            sums = (jnp.zeros(tile, jnp.float32),) * 3
             for x in range(4):
                 for z in range(4):
                     one = e1[u, x + 2, z + 2]
@@ -289,14 +296,16 @@
                         step(e2.at[2 * i + u], energy.at[u], (x + 1, z + 1), (x + 2, z + 2)) - one
                     )
                     e3[2 * i + u, x, z] = three
-                    sign = e0[u, x + 3, z + 3]
-                    sums = [acc + sign * v for acc, v in zip(sums, (one, two, three))]
-        return tuple(sums)
-
-    sums = lax.fori_loop(0, count // 2, interfaces, (jnp.zeros(tile, jnp.float32),) * 3)
-
-    here = 2 * lax.axis_index("ya") + lax.axis_index("yb")
-    before = (here + count - 1) % count
+                    sums = add_sums(sums, e0.at[u], x, z, (one, two, three))
+            for n in range(3):
+                partial[(first + 2 * i + u) % count, n] = sums[n]
+
+        @pl.when(i == 0)
+        def _():
+            lax.fori_loop(0, NX, merge, 0)
+
+        return carry
+
     right = lane % 16 < 6
     outside = (lane < 3) | (lane >= NY - 3)
     rows = blocks.reshape(2 * NX * PROBES * PITCH, NY)
@@ -311,8 +320,8 @@
             for j in range(4):
                 fix = jnp.where(
                     right,
-                    edge[here, x + margin, j + margin],
-                    edge[before, x + margin, j + margin],
+                    edge[1, x + margin, j + margin],
+                    edge[0, x + margin, j + margin],
                 )
                 for w in range(NW):
                     z = 4 * w + j
@@ -323,8 +332,8 @@
             copy_out(n, x).start()
         return carry
 
-    lax.fori_loop(0, NX, merge, 0)
-
+    lax.fori_loop(0, count // 2, interfaces, 0)
+    sums = [sum((partial[k, n] for k in range(1, count)), partial[0, n]) for n in range(3)]
     row = sums_row(sums, (lane % 16 >= 3) & (lane % 16 < 9), probe, lane)
     for k in range(count):
         at = 2 * ROWS * k + PLANES
@@ -337,17 +346,35 @@
             copy_out(n, x).wait()
 
 
+def moment_kernel(parts, moments, *, scale):
+    row = jnp.sum(parts[...], axis=0, keepdims=True) * scale
+    for n in range(3):
+        moments[n : n + 1, :] = pltpu.roll(row, (-8 * n) % NY, 1)[:, :PROBES]
+
+
 def local(rows, dtype=jnp.int32):
     return pltpu.VMEM(rows, dtype)
 
 
 def keep(array):
     return pltpu.with_memory_space_constraint(array, pltpu.VMEM)
+
+
+def far(array):
+    return pltpu.with_memory_space_constraint(array, pltpu.HBM)
 
 
 def shift(array, axis, by):
     count = lax.axis_size(axis)
     return lax.ppermute(array, axis, [(i, (i + by) % count) for i in range(count)])
+
+
+def groups():
+    sizes = [lax.axis_size(axis) for axis in EVERY]
+    found = {}
+    for index, (xa, xb, ya, yb, za, zb) in enumerate(itertools.product(*map(range, sizes))):
+        found.setdefault(((ya + zb) % sizes[2], yb), []).append(((xa, xb, za, zb), index))
+    return [[index for _, index in sorted(members)] for members in found.values()]
 
 
 def per_device(bits, levels):
@@ -361,7 +388,7 @@
         scratch_shapes=[pltpu.SemaphoreType.DMA((2,))],
         name="face",
         compiler_params=SMALL,
-    )(bits, levels)
+    )(far(bits), far(levels))
     bits, levels = keep(bits), keep(levels)
     size = lax.axis_size(GX)
     across = [(i, (i + 1) % size if i % 2 else (i - 1) % size) for i in range(size)]
@@ -426,14 +453,22 @@
             edge(2, 2),
             edge(count, 1),
             edge(count, 0),
+            pltpu.VMEM((count, 3, PROBES, NY), f32),
             pltpu.VMEM((2, NX, PROBES, PITCH, NY), f32),
             pltpu.SemaphoreType.DMA((2, NX)),
         ],
         name="edges",
         compiler_params=SMALL,
     )(gathered, keep(v2), keep(v3))
-    summed = jnp.sum(lax.all_to_all(message, REST, 0, 0, tiled=True), axis=0)
-    moments = summed[: 3 * PROBES].reshape(3, PROBES) / total
+    parts = lax.all_to_all(message, EVERY, 0, 0, axis_index_groups=groups(), tiled=True)
+    moments = pl.pallas_call(
+        functools.partial(moment_kernel, scale=1.0 / total),
+        out_shape=jax.ShapeDtypeStruct((3, PROBES), f32),
+        in_specs=vmem(1),
+        out_specs=vmem(1)[0],
+        name="moment",
+        compiler_params=SMALL,
+    )(keep(parts))
     return moments, previous, current
 
 

time: 64.6 us -> 63.4 us (0.981)
  local copies, waits for them, and re-layouts: 2.09 us -> 0 us
  Pallas kernels: 5.02 us -> 5.86 us
    unnamed x4 -> x0, local copies, waits for them, and re-layouts: 1.43 us -> none
    pallas_call x1, Pallas kernels: 0.05 us -> 0.76 us  [per_device(): pl.pallas_call(face_kernel, out_shape=(local(face), local(face), local(bi...]
    pallas_call x0 -> x1, Pallas kernels: none -> 0.67 us  [per_device(): pl.pallas_call(functools.partial(moment_kernel, scale=1.0 / total), out_s...]
    div x1 -> x0, local copies, waits for them, and re-layouts: 0.66 us -> none  [per_device(): moments = summed[:3 * PROBES].reshape(3, PROBES) / total]
where the time goes in v5:
time: 63.4 us; the launch traced here: 63 us
  blocking collectives  35.5 us (56%)
  starting transfers between devices  21 us (33%)
  Pallas kernels  5.86 us (9%)
  between operations  0.71 us (1%)
    all_to_all x1, blocking collectives, per_device(): lax.all_to_all(message, EVERY, 0, 0, axis_index_groups=groups(), tiled=True)  24.5 us
    ppermute x1, starting transfers between devices, per_device(): odd = keep(lax.ppermute(odd, GX, across))  11.5 us
    ppermute x2, starting transfers between devices, shift(): lax.ppermute(array, axis, [(i, (i + by) % count) for i in range(count)])  9.48 us
    all_gather x1, blocking collectives, per_device(): gathered = keep(lax.all_gather(strips, GY, tiled=True))  7.71 us
    all_gather x1, blocking collectives, per_device(): even = keep(lax.all_gather(even, 'xb', tiled=True))  3.3 us
    pallas_call x1, Pallas kernels, per_device(): pl.pallas_call(inner_kernel, out_shape=(local((ROWS, NY)), local((3, PROB...  2.07 us
    pallas_call x1, Pallas kernels, per_device(): pl.pallas_call(edge_kernel, out_shape=(jax.ShapeDtypeStruct(block, f32),...  1.95 us
  transfers between devices with their start and end apart: 3, of which 0 were waited for; matrix products, arithmetic and copies ran while one was open for 0% of the time, Pallas kernels for 3%

profile of v5, /device:TPU:1, one launch (start us, length us, event | category | flops | bytes accessed | tf_op | source)
XLA Modules:
  0.0 63.0 jit_solution(3835692987979553407)
XLA Ops:
  0.6 0.8 %face.1 = (s32[40,128]{1,0:T(8,128)S(1)}, s32[40,128]{1,0:T(8,128)S(1)}, s32[4,8,128]{2,1,0:T(8,128)S(1)}, s32[4,8,128]{2,1,0:T(8,128)S(1)}) custom-call(s32[4,8,128]{2,1,0:T(8,128)} %bits_far.1, s32[4,8,128]{2,1,0:T(8,128)} %levels_far.1), custom_call_target="tpu_custom_call" | custom-call | tf_op jit(solution)/shard_map/face/pallas_call | solution.py:383
  1.4 11.5 %collective-permute-start = (s32[40,128]{1,0:T(8,128)S(1)}, s32[40,128]{1,0:T(8,128)S(1)}, u32[]{:S(2)}, u32[]{:S(2)}) collective-permute-start(s32[40,128]{1,0:T(8,128)S(1)} %get-tuple-element.27), channel_id=1, source_target_pairs={{0,448},{64,128},{128,64},{192,256},{256,192},{320,384},{384,320},... | collective-permute-start | bytes 61448 | tf_op jit(solution)/shard_map/ppermute | solution.py:395
  12.9 3.3 %all_gather.6.even = s32[80,128]{1,0:T(8,128)S(1)} all-gather(s32[40,128]{1,0:T(8,128)S(1)} %get-tuple-element.26), channel_id=1, replica_groups=mesh['xa'=4,'xb'=2,'ya'=2,'yb'=2,'za'=8,'zb'=2] {'xb'}, dimensions={0}, use_global_device_ids=true | all-gather | bytes 61440 | tf_op jit(solution)/shard_map/all_gather | solution.py:396
  16.2 0.0 collective-permute-done.odd
  16.2 4.7 %collective-permute-start.1 = (s32[24,128]{1,0:T(8,128)S(1)}, s32[24,128]{1,0:T(8,128)S(1)}, u32[]{:S(2)}, u32[]{:S(2)}) collective-permute-start(s32[24,128]{1,0:T(8,128)S(1)} %get-tuple-element.28), channel_id=1, source_target_pairs={{0,1},{1,2},{2,3},{3,4},{4,5},{5,6},{6,7},{7,8},{8,9},{9,10},{10,1... | collective-permute-start | bytes 36872 | tf_op jit(solution)/shard_map/ppermute | solution.py:369
  20.9 4.8 %collective-permute-start.2 = (s32[24,128]{1,0:T(8,128)S(1)}, s32[24,128]{1,0:T(8,128)S(1)}, u32[]{:S(2)}, u32[]{:S(2)}) collective-permute-start(s32[24,128]{1,0:T(8,128)S(1)} %get-tuple-element.29), channel_id=1, source_target_pairs={{0,15},{1,0},{2,1},{3,2},{4,3},{5,4},{6,5},{7,6},{8,7},{9,8},{10,9... | collective-permute-start | bytes 36872 | tf_op jit(solution)/shard_map/ppermute | solution.py:369
  25.7 2.1 %inner.1 = (s32[24,128]{1,0:T(8,128)S(1)}, f32[3,8,128]{2,1,0:T(8,128)S(1)}, f32[10,38,8,128]{3,2,1,0:T(8,128)S(1)}, f32[8,36,8,128]{3,2,1,0:T(8,128)S(1)}, f32[...) custom-call(s32[4,8,128]{2,1,0:T(8,128)S(1)} %get-tuple-element.24.bits, ...), custom_call_target="tpu_custom_call" | custom-call | tf_op jit(solution)/shard_map/inner/pallas_call | solution.py:412
  27.8 0.0 collective-permute-done.1.under
  27.8 0.0 collective-permute-done.2.over
  27.8 0.4 outer.1
  28.2 7.7 %all_gather.7.gathered = s32[192,128]{1,0:T(8,128)S(1)} all-gather(s32[48,128]{1,0:T(8,128)S(1)} %get-tuple-element.39), channel_id=1, replica_groups=mesh['xa'=4,'xb'=2,'ya'=2,'yb'=2,'za'=8,'zb'=2] {'ya','yb'}, dimensions={0}, use_global_device_ids=true | all-gather | bytes 122880 | tf_op jit(solution)/shard_map/all_gather | solution.py:430
  35.9 1.9 %edges.1 = (f32[8,4,32,128]{3,2,1,0:T(8,128)}, f32[8,4,32,128]{3,2,1,0:T(8,128)}, f32[128,128]{1,0:T(8,128)S(1)}) custom-call(s32[192,128]{1,0:T(8,128)S(1)} %all_gather.7.gathered, f32[6,34,8,128]{3,2,1,0:T(8,128)S(1)} %get-tuple-element.40.v2, f32[4,32,8,128]{3,2,1,0:T(8,128)S(1)} %get-tuple-element.41.v3), custom_call_target="tpu_custom_call" | custom-call | tf_op jit(solution)/shard_map/edges/pallas_call | solution.py:440
  37.9 24.5 %all_to_all.11 = f32[128,1,128]{2,1,0:T(1,128)S(1)} all-to-all(f32[128,1,128]{2,1,0:T(1,128)S(1)} %bitcast.5), channel_id=1, replica_groups={{0,33,2,35,4,37,6,39,8,41,10,43,12,45,14,47,64,97,66,99,68,101,70,103,7..., dimensions={0} | all-to-all | bytes 131072 | tf_op jit(solution)/shard_map/all_to_all | solution.py:463
  62.4 0.7 %moment.1 = f32[3,8]{1,0:T(4,128)} custom-call(f32[128,128]{1,0:T(8,128)S(1)} %bitcast.4), custom_call_target="tpu_custom_call" | custom-call | tf_op jit(solution)/shard_map/moment/pallas_call | solution.py:464
  (1 shorter events, 0.0 us)
Async XLA Ops:
  1.4 14.8 %collective-permute-start = (s32[40,128]{1,0:T(8,128)S(1)}, s32[40,128]{1,0:T(8,128)S(1)}, u32[]{:S(2)}, u32[]{:S(2)}) collective-permute-start(s32[40,128]{1,0:T(8,128)S(1)} %get-tuple-element.27), channel_id=1, source_target_pairs={{0,448},{64,128},{128,64},{192,256},{256,192},{320,384},{384,320},... | collective-permute-start | bytes 61448 | tf_op jit(solution)/shard_map/ppermute | solution.py:395
  16.2 11.6 %collective-permute-start.1 = (s32[24,128]{1,0:T(8,128)S(1)}, s32[24,128]{1,0:T(8,128)S(1)}, u32[]{:S(2)}, u32[]{:S(2)}) collective-permute-start(s32[24,128]{1,0:T(8,128)S(1)} %get-tuple-element.28), channel_id=1, source_target_pairs={{0,1},{1,2},{2,3},{3,4},{4,5},{5,6},{6,7},{7,8},{8,9},{9,10},{10,1... | collective-permute-start | bytes 36872 | tf_op jit(solution)/shard_map/ppermute | solution.py:369
  20.9 6.9 %collective-permute-start.2 = (s32[24,128]{1,0:T(8,128)S(1)}, s32[24,128]{1,0:T(8,128)S(1)}, u32[]{:S(2)}, u32[]{:S(2)}) collective-permute-start(s32[24,128]{1,0:T(8,128)S(1)} %get-tuple-element.29), channel_id=1, source_target_pairs={{0,15},{1,0},{2,1},{3,2},{4,3},{5,4},{6,5},{7,6},{8,7},{9,8},{10,9... | collective-permute-start | bytes 36872 | tf_op jit(solution)/shard_map/ppermute | solution.py:369

commit v6 on v5

--- a/solution.py
+++ b/solution.py
@@ -90,7 +90,7 @@
     return ref[at + w : at + w + 1, :]
 
 
-def level_kernel(bits, levels, even, odd, below, above, low, high):
+def level_kernel(bits, levels, even, odd, below, above, z_even, z_odd, low, high):
     upper = lax.axis_index("xb")
     near, far = even[pl.ds(40 * (1 - upper), 40), :], odd[...]
     below[...] = jnp.where(upper == 1, near, far)
@@ -100,6 +100,9 @@
         out[16:24] = jnp.zeros((8, NY), jnp.int32)
         for k, plane in enumerate(planes):
             out[k : k + 1] = word_row(plane, w)
+    up = lax.axis_index("zb") == 0
+    z_even[...] = jnp.where(up, high[...], low[...])
+    z_odd[...] = jnp.where(up, low[...], high[...])
 
 
 def tiles():
@@ -193,9 +196,13 @@
 
 
 def outer_kernel(
-    under, over, strips_in, sums_in, v0_in, energy_in, v1_in, v2_in, v3_in,
+    z_even, z_odd, strips_in, sums_in, v0_in, energy_in, v1_in, v2_in, v3_in,
     strips, v0, energy, v1, v2, v3,
+    under, over,
 ):
+    up = lax.axis_index("zb") == 0
+    under[...] = jnp.where(up, z_odd[...], z_even[...])
+    over[...] = jnp.where(up, z_even[...], z_odd[...])
     del v0_in, energy_in, v1_in, v2_in, v3_in
     tile, probe, lane, bit_of = tiles()
     strips[:ROWS] = strips_in[...]
@@ -364,16 +371,18 @@
     return pltpu.with_memory_space_constraint(array, pltpu.HBM)
 
 
-def shift(array, axis, by):
-    count = lax.axis_size(axis)
-    return lax.ppermute(array, axis, [(i, (i + by) % count) for i in range(count)])
+def across(axis):
+    size = lax.axis_size(axis)
+    return [(i, (i + 1) % size if i % 2 else (i - 1) % size) for i in range(size)]
 
 
 def groups():
     sizes = [lax.axis_size(axis) for axis in EVERY]
     found = {}
     for index, (xa, xb, ya, yb, za, zb) in enumerate(itertools.product(*map(range, sizes))):
-        found.setdefault(((ya + zb) % sizes[2], yb), []).append(((xa, xb, za, zb), index))
+        found.setdefault(((ya + zb) % sizes[2], yb), []).append(
+            (((2 * xa + xb + za) % sizes[4], xa, xb, zb), index)
+        )
     return [[index for _, index in sorted(members)] for members in found.values()]
 
 
@@ -390,20 +399,19 @@
         compiler_params=SMALL,
     )(far(bits), far(levels))
     bits, levels = keep(bits), keep(levels)
-    size = lax.axis_size(GX)
-    across = [(i, (i + 1) % size if i % 2 else (i - 1) % size) for i in range(size)]
-    odd = keep(lax.ppermute(odd, GX, across))
+    odd = keep(lax.ppermute(odd, GX, across(GX)))
     even = keep(lax.all_gather(even, "xb", tiled=True))
-    below, above, z_low, z_high = pl.pallas_call(
+    below, above, z_even, z_odd = pl.pallas_call(
         level_kernel,
         out_shape=(local(face),) * 2 + (local((ROWS, NY)),) * 2,
         in_specs=vmem(4),
         out_specs=tuple(vmem(4)),
+        scratch_shapes=[pltpu.VMEM((ROWS, NY), jnp.int32)] * 2,
         name="level",
         compiler_params=SMALL,
     )(bits, levels, even, odd)
-    under = keep(shift(z_high, GZ, 1))
-    over = keep(shift(z_low, GZ, -1))
+    z_odd = keep(lax.ppermute(z_odd, GZ, across(GZ)))
+    z_even = keep(lax.ppermute(z_even, "zb", [(0, 1), (1, 0)]))
 
     def field(margin):
         return local((NX + 2 * margin, NZ + 2 * margin, PROBES, NY), f32)
@@ -424,9 +432,10 @@
         in_specs=vmem(9),
         out_specs=tuple(vmem(6)),
         input_output_aliases={4 + i: 1 + i for i in range(5)},
+        scratch_shapes=[pltpu.VMEM((ROWS, NY), jnp.int32)] * 2,
         name="outer",
         compiler_params=SMALL,
-    )(under, over, *inner)
+    )(z_even, z_odd, *inner)
     gathered = keep(lax.all_gather(strips, GY, tiled=True))
     count = lax.axis_size(GY)
     rest = lax.axis_size(REST)

time: 63.4 us -> 62.5 us (0.986)
  blocking collectives: 35.5 us -> 33.4 us
  waiting for transfers between devices: 0.01 us -> 0.93 us
    all_to_all x1, blocking collectives: 24.5 us -> 21.5 us  [per_device(): lax.all_to_all(message, EVERY, 0, 0, axis_index_groups=groups(), tiled=True)]
    all_gather x1, blocking collectives: 7.71 us -> 8.7 us  [per_device(): gathered = keep(lax.all_gather(strips, GY, tiled=True))]
    ppermute x3, waiting for transfers between devices: 0.01 us -> 0.93 us  [the longest x1 0.92 us: per_device(): z_odd = keep(lax.ppermute(z_odd, GZ, across(GZ)))]
  transfers between devices with their start and end apart: 3 -> 3, of which waited for: 0 -> 1; matrix products, arithmetic and copies ran while one was open for 0% -> 0% of each run, Pallas kernels for 3% -> 3%
where the time goes in v6:
time: 62.5 us; the launch traced here: 62.1 us
  blocking collectives  33.4 us (53%)
  starting transfers between devices  21.2 us (34%)
  Pallas kernels  5.86 us (9%)
  waiting for transfers between devices  0.93 us (1%)
  between operations  0.7 us (1%)
    all_to_all x1, blocking collectives, per_device(): lax.all_to_all(message, EVERY, 0, 0, axis_index_groups=groups(), tiled=True)  21.5 us
    ppermute x1, starting transfers between devices, per_device(): odd = keep(lax.ppermute(odd, GX, across(GX)))  11.5 us
    all_gather x1, blocking collectives, per_device(): gathered = keep(lax.all_gather(strips, GY, tiled=True))  8.7 us
    ppermute x1, starting transfers between devices, per_device(): z_odd = keep(lax.ppermute(z_odd, GZ, across(GZ)))  5.04 us
    ppermute x1, starting transfers between devices, per_device(): z_even = keep(lax.ppermute(z_even, 'zb', [(0, 1), (1, 0)]))  4.65 us
    all_gather x1, blocking collectives, per_device(): even = keep(lax.all_gather(even, 'xb', tiled=True))  3.3 us
    pallas_call x1, Pallas kernels, per_device(): pl.pallas_call(inner_kernel, out_shape=(local((ROWS, NY)), local((3, PROB...  2.07 us
    pallas_call x1, Pallas kernels, per_device(): pl.pallas_call(edge_kernel, out_shape=(jax.ShapeDtypeStruct(block, f32),...  1.95 us
  transfers between devices with their start and end apart: 3, of which 1 were waited for; matrix products, arithmetic and copies ran while one was open for 0% of the time, Pallas kernels for 3%

profile of v6, /device:TPU:1, one launch (start us, length us, event | category | flops | bytes accessed | tf_op | source)
XLA Modules:
  0.0 62.1 jit_solution(12681865806171122485)
XLA Ops:
  0.6 0.8 %face.1 = (s32[40,128]{1,0:T(8,128)S(1)}, s32[40,128]{1,0:T(8,128)S(1)}, s32[4,8,128]{2,1,0:T(8,128)S(1)}, s32[4,8,128]{2,1,0:T(8,128)S(1)}) custom-call(s32[4,8,128]{2,1,0:T(8,128)} %bits_far.1, s32[4,8,128]{2,1,0:T(8,128)} %levels_far.1), custom_call_target="tpu_custom_call" | custom-call | tf_op jit(solution)/shard_map/face/pallas_call | solution.py:392
  1.4 11.5 %collective-permute-start = (s32[40,128]{1,0:T(8,128)S(1)}, s32[40,128]{1,0:T(8,128)S(1)}, u32[]{:S(2)}, u32[]{:S(2)}) collective-permute-start(s32[40,128]{1,0:T(8,128)S(1)} %get-tuple-element.27), channel_id=1, source_target_pairs={{0,448},{64,128},{128,64},{192,256},{256,192},{320,384},{384,320},... | collective-permute-start | bytes 61448 | tf_op jit(solution)/shard_map/ppermute | solution.py:402
  12.9 3.3 %all_gather.6.even = s32[80,128]{1,0:T(8,128)S(1)} all-gather(s32[40,128]{1,0:T(8,128)S(1)} %get-tuple-element.26), channel_id=1, replica_groups=mesh['xa'=4,'xb'=2,'ya'=2,'yb'=2,'za'=8,'zb'=2] {'xb'}, dimensions={0}, use_global_device_ids=true | all-gather | bytes 61440 | tf_op jit(solution)/shard_map/all_gather | solution.py:403
  16.2 0.0 collective-permute-done.odd
  16.2 4.7 %collective-permute-start.1 = (s32[24,128]{1,0:T(8,128)S(1)}, s32[24,128]{1,0:T(8,128)S(1)}, u32[]{:S(2)}, u32[]{:S(2)}) collective-permute-start(s32[24,128]{1,0:T(8,128)S(1)} %get-tuple-element.28), channel_id=1, source_target_pairs={{0,1},{1,0},{2,3},{3,2},{4,5},{5,4},{6,7},{7,6},{8,9},{9,8},{10,11... | collective-permute-start | bytes 36872 | tf_op jit(solution)/shard_map/ppermute | solution.py:414
  20.9 5.0 %collective-permute-start.2 = (s32[24,128]{1,0:T(8,128)S(1)}, s32[24,128]{1,0:T(8,128)S(1)}, u32[]{:S(2)}, u32[]{:S(2)}) collective-permute-start(s32[24,128]{1,0:T(8,128)S(1)} %get-tuple-element.29), channel_id=1, source_target_pairs={{0,15},{1,2},{2,1},{3,4},{4,3},{5,6},{6,5},{7,8},{8,7},{9,10},{10,... | collective-permute-start | bytes 36872 | tf_op jit(solution)/shard_map/ppermute | solution.py:413
  25.9 2.1 %inner.1 = (s32[24,128]{1,0:T(8,128)S(1)}, f32[3,8,128]{2,1,0:T(8,128)S(1)}, f32[10,38,8,128]{3,2,1,0:T(8,128)S(1)}, f32[8,36,8,128]{3,2,1,0:T(8,128)S(1)}, f32[...) custom-call(s32[4,8,128]{2,1,0:T(8,128)S(1)} %get-tuple-element.24.bits, ...), custom_call_target="tpu_custom_call" | custom-call | tf_op jit(solution)/shard_map/inner/pallas_call | solution.py:420
  28.0 0.0 collective-permute-done.1.z_even
  28.0 0.9 %collective-permute-done.2.z_odd = s32[24,128]{1,0:T(8,128)S(1)} collective-permute-done((s32[24,128]{1,0:T(8,128)S(1)}, s32[24,128]{1,0:T(8,128)S(1)}, u32[]{:S(2)}, u32[]{:S(2)}) %collective-permute-start.2) | collective-permute-done | bytes 12320 | tf_op jit(solution)/shard_map/ppermute | solution.py:413
  28.9 0.4 outer.1
  29.3 8.7 %all_gather.7.gathered = s32[192,128]{1,0:T(8,128)S(1)} all-gather(s32[48,128]{1,0:T(8,128)S(1)} %get-tuple-element.39), channel_id=1, replica_groups=mesh['xa'=4,'xb'=2,'ya'=2,'yb'=2,'za'=8,'zb'=2] {'ya','yb'}, dimensions={0}, use_global_device_ids=true | all-gather | bytes 122880 | tf_op jit(solution)/shard_map/all_gather | solution.py:439
  38.0 1.9 %edges.1 = (f32[8,4,32,128]{3,2,1,0:T(8,128)}, f32[8,4,32,128]{3,2,1,0:T(8,128)}, f32[128,128]{1,0:T(8,128)S(1)}) custom-call(s32[192,128]{1,0:T(8,128)S(1)} %all_gather.7.gathered, f32[6,34,8,128]{3,2,1,0:T(8,128)S(1)} %get-tuple-element.40.v2, f32[4,32,8,128]{3,2,1,0:T(8,128)S(1)} %get-tuple-element.41.v3), custom_call_target="tpu_custom_call" | custom-call | tf_op jit(solution)/shard_map/edges/pallas_call | solution.py:449
  40.0 21.5 %all_to_all.11 = f32[128,1,128]{2,1,0:T(1,128)S(1)} all-to-all(f32[128,1,128]{2,1,0:T(1,128)S(1)} %bitcast.5), channel_id=1, replica_groups={{0,33,78,111,140,173,202,235,264,297,326,359,388,421,450,483,2,35,64,97..., dimensions={0} | all-to-all | bytes 131072 | tf_op jit(solution)/shard_map/all_to_all | solution.py:472
  61.4 0.7 %moment.1 = f32[3,8]{1,0:T(4,128)} custom-call(f32[128,128]{1,0:T(8,128)S(1)} %bitcast.4), custom_call_target="tpu_custom_call" | custom-call | tf_op jit(solution)/shard_map/moment/pallas_call | solution.py:473
  (1 shorter events, 0.0 us)
Async XLA Ops:
  1.4 14.8 %collective-permute-start = (s32[40,128]{1,0:T(8,128)S(1)}, s32[40,128]{1,0:T(8,128)S(1)}, u32[]{:S(2)}, u32[]{:S(2)}) collective-permute-start(s32[40,128]{1,0:T(8,128)S(1)} %get-tuple-element.27), channel_id=1, source_target_pairs={{0,448},{64,128},{128,64},{192,256},{256,192},{320,384},{384,320},... | collective-permute-start | bytes 61448 | tf_op jit(solution)/shard_map/ppermute | solution.py:402
  16.2 11.8 %collective-permute-start.1 = (s32[24,128]{1,0:T(8,128)S(1)}, s32[24,128]{1,0:T(8,128)S(1)}, u32[]{:S(2)}, u32[]{:S(2)}) collective-permute-start(s32[24,128]{1,0:T(8,128)S(1)} %get-tuple-element.28), channel_id=1, source_target_pairs={{0,1},{1,0},{2,3},{3,2},{4,5},{5,4},{6,7},{7,6},{8,9},{9,8},{10,11... | collective-permute-start | bytes 36872 | tf_op jit(solution)/shard_map/ppermute | solution.py:414
  20.9 8.1 %collective-permute-start.2 = (s32[24,128]{1,0:T(8,128)S(1)}, s32[24,128]{1,0:T(8,128)S(1)}, u32[]{:S(2)}, u32[]{:S(2)}) collective-permute-start(s32[24,128]{1,0:T(8,128)S(1)} %get-tuple-element.29), channel_id=1, source_target_pairs={{0,15},{1,2},{2,1},{3,4},{4,3},{5,6},{6,5},{7,8},{8,7},{9,10},{10,... | collective-permute-start | bytes 36872 | tf_op jit(solution)/shard_map/ppermute | solution.py:413

commit v7 on v6

--- a/solution.py
+++ b/solution.py
@@ -196,7 +196,7 @@
 
 
 def outer_kernel(
-    z_even, z_odd, strips_in, sums_in, v0_in, energy_in, v1_in, v2_in, v3_in,
+    z_odd, z_even, strips_in, sums_in, v0_in, energy_in, v1_in, v2_in, v3_in,
     strips, v0, energy, v1, v2, v3,
     under, over,
 ):
@@ -435,7 +435,7 @@
         scratch_shapes=[pltpu.VMEM((ROWS, NY), jnp.int32)] * 2,
         name="outer",
         compiler_params=SMALL,
-    )(z_even, z_odd, *inner)
+    )(z_odd, z_even, *inner)
     gathered = keep(lax.all_gather(strips, GY, tiled=True))
     count = lax.axis_size(GY)
     rest = lax.axis_size(REST)

time: 62.5 us -> 61.1 us (0.978)
  blocking collectives: 33.4 us -> 31.2 us
  waiting for transfers between devices: 0.93 us -> 1.94 us
    ppermute x1, starting transfers between devices: 4.65 us -> 1.92 us  [per_device(): z_even = keep(lax.ppermute(z_even, 'zb', [(0, 1), (1, 0)]))]
    ppermute x1, starting transfers between devices: 5.04 us -> 7.56 us  [per_device(): z_odd = keep(lax.ppermute(z_odd, GZ, across(GZ)))]
    all_to_all x1, blocking collectives: 21.5 us -> 19.2 us  [per_device(): lax.all_to_all(message, EVERY, 0, 0, axis_index_groups=groups(), tiled=True)]
    ppermute x1, waiting for transfers between devices: 0.01 us -> 1.93 us  [per_device(): z_even = keep(lax.ppermute(z_even, 'zb', [(0, 1), (1, 0)]))]
    ppermute x1, waiting for transfers between devices: 0.92 us -> 0.01 us  [per_device(): z_odd = keep(lax.ppermute(z_odd, GZ, across(GZ)))]
where the time goes in v7:
time: 61.1 us; the launch traced here: 60.7 us
  blocking collectives  31.2 us (51%)
  starting transfers between devices  21 us (34%)
  Pallas kernels  5.86 us (10%)
  waiting for transfers between devices  1.94 us (3%)
  between operations  0.7 us (1%)
    all_to_all x1, blocking collectives, per_device(): lax.all_to_all(message, EVERY, 0, 0, axis_index_groups=groups(), tiled=True)  19.2 us
    ppermute x1, starting transfers between devices, per_device(): odd = keep(lax.ppermute(odd, GX, across(GX)))  11.5 us
    all_gather x1, blocking collectives, per_device(): gathered = keep(lax.all_gather(strips, GY, tiled=True))  8.7 us
    ppermute x1, starting transfers between devices, per_device(): z_odd = keep(lax.ppermute(z_odd, GZ, across(GZ)))  7.56 us
    all_gather x1, blocking collectives, per_device(): even = keep(lax.all_gather(even, 'xb', tiled=True))  3.3 us
    pallas_call x1, Pallas kernels, per_device(): pl.pallas_call(inner_kernel, out_shape=(local((ROWS, NY)), local((3, PROB...  2.07 us
    pallas_call x1, Pallas kernels, per_device(): pl.pallas_call(edge_kernel, out_shape=(jax.ShapeDtypeStruct(block, f32),...  1.95 us
    ppermute x1, waiting for transfers between devices, per_device(): z_even = keep(lax.ppermute(z_even, 'zb', [(0, 1), (1, 0)]))  1.93 us
  transfers between devices with their start and end apart: 3, of which 1 were waited for; matrix products, arithmetic and copies ran while one was open for 0% of the time, Pallas kernels for 3%

profile of v7, /device:TPU:1, one launch (start us, length us, event | category | flops | bytes accessed | tf_op | source)
XLA Modules:
  0.0 60.7 jit_solution(2420113517110255374)
XLA Ops:
  0.6 0.8 %face.1 = (s32[40,128]{1,0:T(8,128)S(1)}, s32[40,128]{1,0:T(8,128)S(1)}, s32[4,8,128]{2,1,0:T(8,128)S(1)}, s32[4,8,128]{2,1,0:T(8,128)S(1)}) custom-call(s32[4,8,128]{2,1,0:T(8,128)} %bits_far.1, s32[4,8,128]{2,1,0:T(8,128)} %levels_far.1), custom_call_target="tpu_custom_call" | custom-call | tf_op jit(solution)/shard_map/face/pallas_call | solution.py:392
  1.4 11.5 %collective-permute-start = (s32[40,128]{1,0:T(8,128)S(1)}, s32[40,128]{1,0:T(8,128)S(1)}, u32[]{:S(2)}, u32[]{:S(2)}) collective-permute-start(s32[40,128]{1,0:T(8,128)S(1)} %get-tuple-element.27), channel_id=1, source_target_pairs={{0,448},{64,128},{128,64},{192,256},{256,192},{320,384},{384,320},... | collective-permute-start | bytes 61448 | tf_op jit(solution)/shard_map/ppermute | solution.py:402
  12.9 3.3 %all_gather.6.even = s32[80,128]{1,0:T(8,128)S(1)} all-gather(s32[40,128]{1,0:T(8,128)S(1)} %get-tuple-element.26), channel_id=1, replica_groups=mesh['xa'=4,'xb'=2,'ya'=2,'yb'=2,'za'=8,'zb'=2] {'xb'}, dimensions={0}, use_global_device_ids=true | all-gather | bytes 61440 | tf_op jit(solution)/shard_map/all_gather | solution.py:403
  16.2 0.0 collective-permute-done.odd
  16.2 7.6 %collective-permute-start.1 = (s32[24,128]{1,0:T(8,128)S(1)}, s32[24,128]{1,0:T(8,128)S(1)}, u32[]{:S(2)}, u32[]{:S(2)}) collective-permute-start(s32[24,128]{1,0:T(8,128)S(1)} %get-tuple-element.28), channel_id=1, source_target_pairs={{0,15},{1,2},{2,1},{3,4},{4,3},{5,6},{6,5},{7,8},{8,7},{9,10},{10,... | collective-permute-start | bytes 36872 | tf_op jit(solution)/shard_map/ppermute | solution.py:413
  23.8 1.9 %collective-permute-start.2 = (s32[24,128]{1,0:T(8,128)S(1)}, s32[24,128]{1,0:T(8,128)S(1)}, u32[]{:S(2)}, u32[]{:S(2)}) collective-permute-start(s32[24,128]{1,0:T(8,128)S(1)} %get-tuple-element.29), channel_id=1, source_target_pairs={{0,1},{1,0},{2,3},{3,2},{4,5},{5,4},{6,7},{7,6},{8,9},{9,8},{10,11... | collective-permute-start | bytes 36872 | tf_op jit(solution)/shard_map/ppermute | solution.py:414
  25.7 2.1 %inner.1 = (s32[24,128]{1,0:T(8,128)S(1)}, f32[3,8,128]{2,1,0:T(8,128)S(1)}, f32[10,38,8,128]{3,2,1,0:T(8,128)S(1)}, f32[8,36,8,128]{3,2,1,0:T(8,128)S(1)}, f32[...) custom-call(s32[4,8,128]{2,1,0:T(8,128)S(1)} %get-tuple-element.24.bits, ...), custom_call_target="tpu_custom_call" | custom-call | tf_op jit(solution)/shard_map/inner/pallas_call | solution.py:420
  27.8 0.0 collective-permute-done.1.z_odd
  27.8 1.9 %collective-permute-done.2.z_even = s32[24,128]{1,0:T(8,128)S(1)} collective-permute-done((s32[24,128]{1,0:T(8,128)S(1)}, s32[24,128]{1,0:T(8,128)S(1)}, u32[]{:S(2)}, u32[]{:S(2)}) %collective-permute-start.2) | collective-permute-done | bytes 12320 | tf_op jit(solution)/shard_map/ppermute | solution.py:414
  29.7 0.4 outer.1
  30.1 8.7 %all_gather.7.gathered = s32[192,128]{1,0:T(8,128)S(1)} all-gather(s32[48,128]{1,0:T(8,128)S(1)} %get-tuple-element.39), channel_id=1, replica_groups=mesh['xa'=4,'xb'=2,'ya'=2,'yb'=2,'za'=8,'zb'=2] {'ya','yb'}, dimensions={0}, use_global_device_ids=true | all-gather | bytes 122880 | tf_op jit(solution)/shard_map/all_gather | solution.py:439
  38.8 1.9 %edges.1 = (f32[8,4,32,128]{3,2,1,0:T(8,128)}, f32[8,4,32,128]{3,2,1,0:T(8,128)}, f32[128,128]{1,0:T(8,128)S(1)}) custom-call(s32[192,128]{1,0:T(8,128)S(1)} %all_gather.7.gathered, f32[6,34,8,128]{3,2,1,0:T(8,128)S(1)} %get-tuple-element.40.v2, f32[4,32,8,128]{3,2,1,0:T(8,128)S(1)} %get-tuple-element.41.v3), custom_call_target="tpu_custom_call" | custom-call | tf_op jit(solution)/shard_map/edges/pallas_call | solution.py:449
  40.8 19.2 %all_to_all.11 = f32[128,1,128]{2,1,0:T(1,128)S(1)} all-to-all(f32[128,1,128]{2,1,0:T(1,128)S(1)} %bitcast.5), channel_id=1, replica_groups={{0,33,78,111,140,173,202,235,264,297,326,359,388,421,450,483,2,35,64,97..., dimensions={0} | all-to-all | bytes 131072 | tf_op jit(solution)/shard_map/all_to_all | solution.py:472
  60.0 0.7 %moment.1 = f32[3,8]{1,0:T(4,128)} custom-call(f32[128,128]{1,0:T(8,128)S(1)} %bitcast.4), custom_call_target="tpu_custom_call" | custom-call | tf_op jit(solution)/shard_map/moment/pallas_call | solution.py:473
  (1 shorter events, 0.0 us)
Async XLA Ops:
  1.4 14.8 %collective-permute-start = (s32[40,128]{1,0:T(8,128)S(1)}, s32[40,128]{1,0:T(8,128)S(1)}, u32[]{:S(2)}, u32[]{:S(2)}) collective-permute-start(s32[40,128]{1,0:T(8,128)S(1)} %get-tuple-element.27), channel_id=1, source_target_pairs={{0,448},{64,128},{128,64},{192,256},{256,192},{320,384},{384,320},... | collective-permute-start | bytes 61448 | tf_op jit(solution)/shard_map/ppermute | solution.py:402
  16.2 11.6 %collective-permute-start.1 = (s32[24,128]{1,0:T(8,128)S(1)}, s32[24,128]{1,0:T(8,128)S(1)}, u32[]{:S(2)}, u32[]{:S(2)}) collective-permute-start(s32[24,128]{1,0:T(8,128)S(1)} %get-tuple-element.28), channel_id=1, source_target_pairs={{0,15},{1,2},{2,1},{3,4},{4,3},{5,6},{6,5},{7,8},{8,7},{9,10},{10,... | collective-permute-start | bytes 36872 | tf_op jit(solution)/shard_map/ppermute | solution.py:413
  23.8 5.9 %collective-permute-start.2 = (s32[24,128]{1,0:T(8,128)S(1)}, s32[24,128]{1,0:T(8,128)S(1)}, u32[]{:S(2)}, u32[]{:S(2)}) collective-permute-start(s32[24,128]{1,0:T(8,128)S(1)} %get-tuple-element.29), channel_id=1, source_target_pairs={{0,1},{1,0},{2,3},{3,2},{4,5},{5,4},{6,7},{7,6},{8,9},{9,8},{10,11... | collective-permute-start | bytes 36872 | tf_op jit(solution)/shard_map/ppermute | solution.py:414

commit v8 on v7

--- a/solution.py
+++ b/solution.py
@@ -162,26 +162,26 @@
                 energy[k, 4 * w + j + 2] = energy_of(row, j)
 
     def first(i, carry):
-        for u in range(2):
-            x = 2 * i + u
+        for u in range(4):
+            x = 4 * i + u
             for z in range(3, NZ + 1):
                 v1[x, z] = 0.5 * step(v0, energy, (x + 1, z + 1), (x, z))
         return carry
 
-    lax.fori_loop(0, (NX + 4) // 2, first, 0)
+    lax.fori_loop(0, (NX + 4) // 4, first, 0)
 
     def second(i, carry):
-        for u in range(2):
-            x = 2 * i + u
+        for u in range(3):
+            x = 3 * i + u
             for z in range(3, NZ - 1):
                 v2[x, z] = step(v1, energy, (x + 1, z + 1), (x + 1, z + 1)) - v0[x + 2, z + 2]
         return carry
 
-    lax.fori_loop(0, (NX + 2) // 2, second, 0)
+    lax.fori_loop(0, (NX + 2) // 3, second, 0)
 
     def third(i, sums):
-        for u in range(2):
-            x = 2 * i + u
+        for u in range(4):
+            x = 4 * i + u
             for z in range(3, NZ - 3):
                 one = v1[x + 2, z + 2]
                 two = v2[x + 1, z + 1]
@@ -190,7 +190,7 @@
                 sums = add_sums(sums, v0, x, z, (one, two, three))
         return tuple(sums)
 
-    sums = lax.fori_loop(0, NX // 2, third, (jnp.zeros(tile, jnp.float32),) * 3)
+    sums = lax.fori_loop(0, NX // 4, third, (jnp.zeros(tile, jnp.float32),) * 3)
     for n in range(3):
         sums_out[n] = sums[n]
 

time: 61.1 us -> 61.1 us (level)
  no operation moved by 1% of the time
where the time goes in v8:
time: 61.1 us; the launch traced here: 60.7 us
  blocking collectives  31.2 us (51%)
  starting transfers between devices  21 us (34%)
  Pallas kernels  5.57 us (9%)
  waiting for transfers between devices  2.23 us (4%)
  between operations  0.69 us (1%)
    all_to_all x1, blocking collectives, per_device(): lax.all_to_all(message, EVERY, 0, 0, axis_index_groups=groups(), tiled=True)  19.2 us
    ppermute x1, starting transfers between devices, per_device(): odd = keep(lax.ppermute(odd, GX, across(GX)))  11.5 us
    all_gather x1, blocking collectives, per_device(): gathered = keep(lax.all_gather(strips, GY, tiled=True))  8.7 us
    ppermute x1, starting transfers between devices, per_device(): z_odd = keep(lax.ppermute(z_odd, GZ, across(GZ)))  7.56 us
    all_gather x1, blocking collectives, per_device(): even = keep(lax.all_gather(even, 'xb', tiled=True))  3.3 us
    ppermute x1, waiting for transfers between devices, per_device(): z_even = keep(lax.ppermute(z_even, 'zb', [(0, 1), (1, 0)]))  2.22 us
    pallas_call x1, Pallas kernels, per_device(): pl.pallas_call(edge_kernel, out_shape=(jax.ShapeDtypeStruct(block, f32),...  1.95 us
    ppermute x1, starting transfers between devices, per_device(): z_even = keep(lax.ppermute(z_even, 'zb', [(0, 1), (1, 0)]))  1.92 us
  transfers between devices with their start and end apart: 3, of which 1 were waited for; matrix products, arithmetic and copies ran while one was open for 0% of the time, Pallas kernels for 3%

profile of v8, /device:TPU:1, one launch (start us, length us, event | category | flops | bytes accessed | tf_op | source)
XLA Modules:
  0.0 60.7 jit_solution(17419876365333049695)
XLA Ops:
  0.6 0.8 %face.1 = (s32[40,128]{1,0:T(8,128)S(1)}, s32[40,128]{1,0:T(8,128)S(1)}, s32[4,8,128]{2,1,0:T(8,128)S(1)}, s32[4,8,128]{2,1,0:T(8,128)S(1)}) custom-call(s32[4,8,128]{2,1,0:T(8,128)} %bits_far.1, s32[4,8,128]{2,1,0:T(8,128)} %levels_far.1), custom_call_target="tpu_custom_call" | custom-call | tf_op jit(solution)/shard_map/face/pallas_call | solution.py:392
  1.4 11.5 %collective-permute-start = (s32[40,128]{1,0:T(8,128)S(1)}, s32[40,128]{1,0:T(8,128)S(1)}, u32[]{:S(2)}, u32[]{:S(2)}) collective-permute-start(s32[40,128]{1,0:T(8,128)S(1)} %get-tuple-element.27), channel_id=1, source_target_pairs={{0,448},{64,128},{128,64},{192,256},{256,192},{320,384},{384,320},... | collective-permute-start | bytes 61448 | tf_op jit(solution)/shard_map/ppermute | solution.py:402
  12.9 3.3 %all_gather.6.even = s32[80,128]{1,0:T(8,128)S(1)} all-gather(s32[40,128]{1,0:T(8,128)S(1)} %get-tuple-element.26), channel_id=1, replica_groups=mesh['xa'=4,'xb'=2,'ya'=2,'yb'=2,'za'=8,'zb'=2] {'xb'}, dimensions={0}, use_global_device_ids=true | all-gather | bytes 61440 | tf_op jit(solution)/shard_map/all_gather | solution.py:403
  16.2 0.0 collective-permute-done.odd
  16.2 7.6 %collective-permute-start.1 = (s32[24,128]{1,0:T(8,128)S(1)}, s32[24,128]{1,0:T(8,128)S(1)}, u32[]{:S(2)}, u32[]{:S(2)}) collective-permute-start(s32[24,128]{1,0:T(8,128)S(1)} %get-tuple-element.28), channel_id=1, source_target_pairs={{0,15},{1,2},{2,1},{3,4},{4,3},{5,6},{6,5},{7,8},{8,7},{9,10},{10,... | collective-permute-start | bytes 36872 | tf_op jit(solution)/shard_map/ppermute | solution.py:413
  23.8 1.9 %collective-permute-start.2 = (s32[24,128]{1,0:T(8,128)S(1)}, s32[24,128]{1,0:T(8,128)S(1)}, u32[]{:S(2)}, u32[]{:S(2)}) collective-permute-start(s32[24,128]{1,0:T(8,128)S(1)} %get-tuple-element.29), channel_id=1, source_target_pairs={{0,1},{1,0},{2,3},{3,2},{4,5},{5,4},{6,7},{7,6},{8,9},{9,8},{10,11... | collective-permute-start | bytes 36872 | tf_op jit(solution)/shard_map/ppermute | solution.py:414
  25.7 1.8 %inner.1 = (s32[24,128]{1,0:T(8,128)S(1)}, f32[3,8,128]{2,1,0:T(8,128)S(1)}, f32[10,38,8,128]{3,2,1,0:T(8,128)S(1)}, f32[8,36,8,128]{3,2,1,0:T(8,128)S(1)}, f32[...) custom-call(s32[4,8,128]{2,1,0:T(8,128)S(1)} %get-tuple-element.24.bits, ...), custom_call_target="tpu_custom_call" | custom-call | tf_op jit(solution)/shard_map/inner/pallas_call | solution.py:420
  27.5 0.0 collective-permute-done.1.z_odd
  27.5 2.2 %collective-permute-done.2.z_even = s32[24,128]{1,0:T(8,128)S(1)} collective-permute-done((s32[24,128]{1,0:T(8,128)S(1)}, s32[24,128]{1,0:T(8,128)S(1)}, u32[]{:S(2)}, u32[]{:S(2)}) %collective-permute-start.2) | collective-permute-done | bytes 12320 | tf_op jit(solution)/shard_map/ppermute | solution.py:414
  29.7 0.4 outer.1
  30.1 8.7 %all_gather.7.gathered = s32[192,128]{1,0:T(8,128)S(1)} all-gather(s32[48,128]{1,0:T(8,128)S(1)} %get-tuple-element.39), channel_id=1, replica_groups=mesh['xa'=4,'xb'=2,'ya'=2,'yb'=2,'za'=8,'zb'=2] {'ya','yb'}, dimensions={0}, use_global_device_ids=true | all-gather | bytes 122880 | tf_op jit(solution)/shard_map/all_gather | solution.py:439
  38.8 1.9 %edges.1 = (f32[8,4,32,128]{3,2,1,0:T(8,128)}, f32[8,4,32,128]{3,2,1,0:T(8,128)}, f32[128,128]{1,0:T(8,128)S(1)}) custom-call(s32[192,128]{1,0:T(8,128)S(1)} %all_gather.7.gathered, f32[6,34,8,128]{3,2,1,0:T(8,128)S(1)} %get-tuple-element.40.v2, f32[4,32,8,128]{3,2,1,0:T(8,128)S(1)} %get-tuple-element.41.v3), custom_call_target="tpu_custom_call" | custom-call | tf_op jit(solution)/shard_map/edges/pallas_call | solution.py:449
  40.8 19.2 %all_to_all.11 = f32[128,1,128]{2,1,0:T(1,128)S(1)} all-to-all(f32[128,1,128]{2,1,0:T(1,128)S(1)} %bitcast.5), channel_id=1, replica_groups={{0,33,78,111,140,173,202,235,264,297,326,359,388,421,450,483,2,35,64,97..., dimensions={0} | all-to-all | bytes 131072 | tf_op jit(solution)/shard_map/all_to_all | solution.py:472
  60.0 0.7 %moment.1 = f32[3,8]{1,0:T(4,128)} custom-call(f32[128,128]{1,0:T(8,128)S(1)} %bitcast.4), custom_call_target="tpu_custom_call" | custom-call | tf_op jit(solution)/shard_map/moment/pallas_call | solution.py:473
  (1 shorter events, 0.0 us)
Async XLA Ops:
  1.4 14.8 %collective-permute-start = (s32[40,128]{1,0:T(8,128)S(1)}, s32[40,128]{1,0:T(8,128)S(1)}, u32[]{:S(2)}, u32[]{:S(2)}) collective-permute-start(s32[40,128]{1,0:T(8,128)S(1)} %get-tuple-element.27), channel_id=1, source_target_pairs={{0,448},{64,128},{128,64},{192,256},{256,192},{320,384},{384,320},... | collective-permute-start | bytes 61448 | tf_op jit(solution)/shard_map/ppermute | solution.py:402
  16.2 11.3 %collective-permute-start.1 = (s32[24,128]{1,0:T(8,128)S(1)}, s32[24,128]{1,0:T(8,128)S(1)}, u32[]{:S(2)}, u32[]{:S(2)}) collective-permute-start(s32[24,128]{1,0:T(8,128)S(1)} %get-tuple-element.28), channel_id=1, source_target_pairs={{0,15},{1,2},{2,1},{3,4},{4,3},{5,6},{6,5},{7,8},{8,7},{9,10},{10,... | collective-permute-start | bytes 36872 | tf_op jit(solution)/shard_map/ppermute | solution.py:413
  23.8 5.9 %collective-permute-start.2 = (s32[24,128]{1,0:T(8,128)S(1)}, s32[24,128]{1,0:T(8,128)S(1)}, u32[]{:S(2)}, u32[]{:S(2)}) collective-permute-start(s32[24,128]{1,0:T(8,128)S(1)} %get-tuple-element.29), channel_id=1, source_target_pairs={{0,1},{1,0},{2,3},{3,2},{4,5},{5,4},{6,7},{7,6},{8,9},{9,8},{10,11... | collective-permute-start | bytes 36872 | tf_op jit(solution)/shard_map/ppermute | solution.py:414
